TPU v7x, 256 devices: a whole 4x4x8 slice. The times are simulated.
256 devices in a mesh: tile: 32 (over y, z), cplx: 8 (over x, core).
Axes of the slice: x: 4, y: 4, z: 8, core: 2. Of those that a mesh axis runs over, the one named last changes fastest.
Arguments:
- pair_tiles: bfloat16 [768, 128, 128, 128], P(('tile', 'cplx'))
- tile_map: int32 [768, 3], replicated, may hold values from -1 to 47, as said below
- lengths: int32 [48], replicated, may hold values from 256 to 512
- resolved: int32 [48, 512], replicated, may hold values 0 or 1
- ln_gain: float32 [128], replicated, may hold values from 0.1 to 1.9
- w_in: bfloat16 [128, 512], replicated, may hold values from -0.5 to 0.5
- w_out: bfloat16 [512, 128], replicated, may hold values from -0.25 to 0.25
- w_head: bfloat16 [128, 64], replicated
- head_bias: float32 [64], replicated, may hold values from -4 to 4
Outputs:
- error_map: float32 [48, 512, 512], P('cplx', 'tile')
- residue_error: float32 [48, 512], P('cplx', 'tile')
- tm_score: float32 [48], P('cplx')
Inputs may be any that keep to these rules, and one draw needn't show every extreme that they name: `tile_map`: row (t * 8 + c) * 3 + j is slot j of the device at tile index t and cplx index c and holds the complex, block row and block column of its tile, or -1 three times where the slot is empty. Each tile (k, r, q) with r and q below ceil(lengths[k] / 128) is held by exactly one slot and no other tile is held. Complex k is owned by cplx index k // 6; no two filled slots of one device have the same owner, and for fixed t and j the owners over the 8 cplx indices are all different.
All inputs are finite; a program needn't handle non-finite values.
Results may differ from a plain program's by a relative error of at most 0.0089.
Values sent between devices are 32-bit elements; how exact they have to be, the bound alone decides.
A program may use at most 128 MiB of HBM per device.

v0:
```python
import jax
import jax.numpy as jnp
from jax import lax
from jax.sharding import PartitionSpec as P

EPS = 1e-05


def in_one_piece(arrays, axis, split_dim, concat_dim, along):
    columns = [a.reshape(*a.shape[:along], -1) for a in arrays]
    both = jnp.concatenate(columns, axis=along)
    out, at, finished = (
        lax.all_to_all(both, axis, split_axis=split_dim, concat_axis=concat_dim, tiled=True),
        0,
        [],
    )
    for a, column in zip(arrays, columns):
        section = out[..., at : at + column.shape[along]]
        finished.append(section.reshape(*section.shape[:along], *a.shape[along:]))
        at += column.shape[along]
    return tuple(finished)


def copy_for_each(array, axis):
    copies = jnp.broadcast_to(array, (lax.axis_size(axis), *array.shape))
    return lax.all_to_all(copies, axis, split_axis=0, concat_axis=0, tiled=True)


def taken_together(array, axis):
    everything = copy_for_each(array, axis)
    return jnp.max(everything, axis=0)


def bin_centers(bin_count):
    bin_step = 31.0 / (bin_count - 2)
    return (jnp.arange(bin_count, dtype=jnp.float32) + 0.5) * bin_step


def d_zero(length):
    clipped = jnp.maximum(length, 19).astype(jnp.float32)
    return 1.24 * jnp.cbrt(clipped - 15.0) - 1.8


def pair_head(row_block, ln_gain, w_in, w_out, w_head, head_bias, centers, distance):
    values = row_block.astype(jnp.float32)
    row_mean = jnp.mean(values, axis=-1, keepdims=True)
    centred = values - row_mean
    variance = jnp.mean(centred * centred, axis=-1, keepdims=True)
    normed = (centred * lax.rsqrt(variance + EPS) * ln_gain).astype(jnp.bfloat16)
    hidden = jax.nn.relu(jnp.dot(normed, w_in, preferred_element_type=jnp.float32)).astype(
        jnp.bfloat16
    )
    updated = (values + jnp.dot(hidden, w_out, preferred_element_type=jnp.float32)).astype(
        jnp.bfloat16
    )
    logits = jnp.dot(updated, w_head, preferred_element_type=jnp.float32) + head_bias
    bin_probs = jax.nn.softmax(logits, axis=-1)
    expected = jnp.sum(bin_probs * centers, axis=-1)
    tm_term = jnp.sum(bin_probs / (1.0 + (centers / distance) ** 2), axis=-1)
    return (expected, tm_term)


def route_rows(
    error_src, rows_src, row_src, found_src, n_tile, parts_per, rows_each, tile_side, highest
):
    target_rows = jnp.arange(n_tile, dtype=jnp.int32)[:, None, None]
    part_index = jnp.arange(parts_per, dtype=jnp.int32)[None, None, :]
    routing = (
        (target_rows == row_src[None, :, None] * parts_per + part_index) & found_src[None, :, None]
    ).astype(jnp.float32)
    sender_count = error_src.shape[0]
    error_parts = error_src.reshape(sender_count, parts_per, rows_each, tile_side)
    row_parts = rows_src.reshape(sender_count, parts_per, rows_each)
    error_out = jnp.einsum("tcq,cqrj->tcrj", routing, error_parts, precision=highest)
    rows_out = jnp.einsum("tcq,cqr->tcr", routing, row_parts, precision=highest)
    return (error_out, rows_out)


def place_rows(
    error_back,
    rows_back,
    member_all,
    row_all,
    colblk_all,
    found_all,
    row_index,
    parts_per,
    cpx_dev,
    blocks,
    rows_each,
    tile_side,
    maxres,
    highest,
):
    mine_rows = found_all & (row_all == row_index // parts_per)
    member_hot = (
        (jnp.arange(cpx_dev, dtype=jnp.int32)[None, None, :] == member_all[..., None])
        & mine_rows[..., None]
    ).astype(jnp.float32)
    block_hot = (
        jnp.arange(blocks, dtype=jnp.int32)[None, None, :] == colblk_all[..., None]
    ).astype(jnp.float32)
    sources = member_all.shape[0] * member_all.shape[1]
    place_hot = (member_hot[..., :, None] * block_hot[..., None, :]).reshape(
        sources, cpx_dev, blocks
    )
    share_map = jnp.einsum(
        "smb,srj->mrbj",
        place_hot,
        error_back.reshape(sources, rows_each, tile_side),
        precision=highest,
    ).reshape(cpx_dev, rows_each, maxres)
    share_rows = jnp.einsum(
        "sm,sr->mr",
        member_hot.reshape(sources, cpx_dev),
        rows_back.reshape(sources, rows_each),
        precision=highest,
    )
    return (share_map, share_rows)


def shards(pair_tiles, tile_map, lengths, resolved, ln_gain, w_in, w_out, w_head, head_bias):
    highest = lax.Precision.HIGHEST
    n_tile = lax.axis_size("tile")
    n_cplx = lax.axis_size("cplx")
    row_index = lax.axis_index("tile")
    col_index = lax.axis_index("cplx")
    slot_count, tile_side, _, pair_width = pair_tiles.shape
    complexes, maxres = resolved.shape
    blocks = maxres // tile_side
    cpx_dev = complexes // n_cplx
    rows_each = maxres // n_tile
    parts_per = tile_side // rows_each
    centers = bin_centers(w_head.shape[1])
    positions = jnp.arange(maxres, dtype=jnp.int32)
    valid_mask = ((positions[None, :] < lengths[:, None]) & (resolved > 0)).astype(jnp.float32)
    valid_blocks = valid_mask.reshape(complexes, blocks, tile_side)
    layout = tile_map.reshape(n_tile, n_cplx, slot_count, 3)
    own_slots = layout[row_index, col_index]
    row_count = tile_side * tile_side
    block_rows = min(4096, row_count)
    error_tiles = []
    score_tiles = []
    owner_list = []
    for slot in range(slot_count):
        slot_meta = own_slots[slot]
        present = slot_meta[0] >= 0
        complex_id = jnp.maximum(slot_meta[0], 0)
        block_row = jnp.maximum(slot_meta[1], 0)
        block_col = jnp.maximum(slot_meta[2], 0)
        distance = d_zero(lengths[complex_id])

        def head_block(row_block, distance=distance):
            return pair_head(row_block, ln_gain, w_in, w_out, w_head, head_bias, centers, distance)

        expected, tm_term = lax.map(
            head_block, pair_tiles[slot].reshape(row_count // block_rows, block_rows, pair_width)
        )
        row_valid = valid_blocks[complex_id, block_row]
        col_valid = valid_blocks[complex_id, block_col]
        weight = jnp.where(present, row_valid[:, None] * col_valid[None, :], jnp.float32(0.0))
        error_tiles.append(weight * expected.reshape(tile_side, tile_side))
        score_tiles.append(weight * tm_term.reshape(tile_side, tile_side))
        owner_list.append(jnp.where(present, complex_id // cpx_dev, -1))
    owner_ids = jnp.stack(owner_list)
    select = (jnp.arange(n_cplx, dtype=jnp.int32)[:, None] == owner_ids[None, :]).astype(
        jnp.float32
    )
    error_send = jnp.einsum("os,sij->oij", select, jnp.stack(error_tiles), precision=highest)
    score_rows = jnp.stack([jnp.sum(score_tile, axis=1) for score_tile in score_tiles])
    score_send = jnp.einsum("os,si->oi", select, score_rows, precision=highest)
    error_in, rows_in = in_one_piece((error_send, score_send), "cplx", 0, 0, 2)
    complex_all = layout[..., 0]
    owner_all = jnp.where(complex_all >= 0, complex_all // cpx_dev, -1)
    matched = owner_all == col_index
    matched_float = matched.astype(jnp.float32)
    slot_hot = matched_float[row_index]
    error_slots = jnp.einsum("sj,sab->jab", slot_hot, error_in, precision=highest)
    rows_slots = jnp.einsum("sj,sa->ja", slot_hot, rows_in, precision=highest)
    found_slot = jnp.any(matched, axis=1)

    def pick_slot(column):
        return jnp.sum(jnp.where(matched, layout[..., column], 0), axis=1)

    member_slot = pick_slot(0) - col_index * cpx_dev
    row_slot = pick_slot(1)
    colblk_slot = pick_slot(2)
    error_out, rows_out = route_rows(
        error_slots,
        rows_slots,
        row_slot[row_index],
        found_slot[row_index],
        n_tile,
        parts_per,
        rows_each,
        tile_side,
        highest,
    )
    error_back, rows_back = (
        lax.all_to_all(error_out, "tile", split_axis=0, concat_axis=0, tiled=True),
        lax.all_to_all(rows_out, "tile", split_axis=0, concat_axis=0, tiled=True),
    )
    share_map, share_rows = place_rows(
        error_back,
        rows_back,
        member_slot,
        row_slot,
        colblk_slot,
        found_slot,
        row_index,
        parts_per,
        cpx_dev,
        blocks,
        rows_each,
        tile_side,
        maxres,
        highest,
    )
    valid_rows = lax.dynamic_slice(
        valid_mask, (col_index * cpx_dev, row_index * rows_each), (cpx_dev, rows_each)
    )
    totals = lax.dynamic_slice_in_dim(jnp.sum(valid_mask, axis=1), col_index * cpx_dev, cpx_dev)
    denominator = jnp.maximum(valid_rows * totals[:, None], jnp.float32(1.0))
    residue_error = jnp.sum(share_map, axis=2) / denominator
    best_share = jnp.max(share_rows / denominator, axis=1)
    tm_score = taken_together(best_share, "tile")
    return (share_map, residue_error, tm_score)


def solution(mesh):
    placed = (P(("tile", "cplx"), None, None, None), P(), P(), P(), P(), P(), P(), P(), P())
    return jax.shard_map(
        shards,
        mesh=mesh,
        in_specs=placed,
        out_specs=(P("cplx", "tile", None), P("cplx", "tile"), P("cplx")),
        check_vma=False,
    )
```

profile of v0, /device:TPU:32, one launch (start us, length us, event | category | flops | bytes accessed | tf_op | source)
XLA Modules:
  0.0 221.8 jit_solution(15761874110064853936)
XLA Ops:
  6.3 8.9 %fusion.150 = (bf16[1,128,128,128]{3,2,1,0:T(8,128)(2,1)}, bf16[1,128,128,128]{3,2,1,0:T(8,128)(2,1)}, bf16[1,128,128,128]{3,2,1,0:T(8,128)(2,1)}) fusion(bf16[3,128,128,128]{3,2,1,0:T(8,128)(2,1)} %param.15), kind=kLoop, calls=%fused_computation.200 | loop fusion | bytes 25165824 | tf_op jit(solution)/shard_map/slice | solution.py:157
  16.6 38.7 %while.44 = (s32[]{:T(128)}, f32[4,4096]{1,0:T(4,128)S(1)}, f32[4,4096]{1,0:T(4,128)S(1)}, bf16[4,4096,128]{2,1,0:T(8,128)(2,1)}, f32[128]{0:T(128)S(1)}, /*inde...) while((s32[]{:T(128)}, f32[4,4096]{1,0:T(4,128)S(1)}, ...), condition=%wide.region_23.24_spmd.clone.clone, body=%wide.region_16.23_spmd.clone.clone.sunk | while | flops 1155256576 | bytes 10046353 | solution.py:156
  18.3 2.3 %fusion.226 = f32[4096]{0:T(1024)S(1)} fusion(f32[4096]{0:T(1024)S(1)} %broadcast_multiply_fusion.8, bf16[4,4096,128]{2,1,0:T(8,128)(2,1)} %get-tuple-element.694, s32[]{:T(128)S(6)} %copy.206), kind=kLoop, calls=%fused_computation.68.clone.1 | loop fusion | flops 2093056 | bytes 1081348 | tf_op jit(solution)/shard_map/while/body/eval_jaxpr/reduce_sum | solution.py:48
  20.6 4.1 %fusion.227 = bf16[4096,128]{1,0:T(8,128)(2,1)S(1)} fusion(bf16[512,128]{1,0:T(8,128)(2,1)S(1)} %get-tuple-element.697, bf16[128,512]{1,0:T(8,128)(2,1)S(1)} %get-tuple-element.696, f32[128]{0:T(128)S(1)} %get-tuple-element.695, f32[4096]{0:T(1024)S(1)} %add_rsqrt_fusion.8, f32[4096]{0:T(1024)S(1)} %broadcast_multiply_fusion.8, ...), kind=kOutput, calls=%fused_computation.61.clone.1 | convolution fusion | flops 1082130432 | bytes 3442176 | tf_op jit(solution)/shard_map/while/body/eval_jaxpr/dot_general | solution.py:53
  28.0 2.3 %fusion.226 = f32[4096]{0:T(1024)S(1)} fusion(f32[4096]{0:T(1024)S(1)} %broadcast_multiply_fusion.8, bf16[4,4096,128]{2,1,0:T(8,128)(2,1)} %get-tuple-element.694, s32[]{:T(128)S(6)} %copy.206), kind=kLoop, calls=%fused_computation.68.clone.1 | loop fusion | flops 2093056 | bytes 1081348 | tf_op jit(solution)/shard_map/while/body/eval_jaxpr/reduce_sum | solution.py:48
  30.4 4.0 %fusion.227 = bf16[4096,128]{1,0:T(8,128)(2,1)S(1)} fusion(bf16[512,128]{1,0:T(8,128)(2,1)S(1)} %get-tuple-element.697, bf16[128,512]{1,0:T(8,128)(2,1)S(1)} %get-tuple-element.696, f32[128]{0:T(128)S(1)} %get-tuple-element.695, f32[4096]{0:T(1024)S(1)} %add_rsqrt_fusion.8, f32[4096]{0:T(1024)S(1)} %broadcast_multiply_fusion.8, ...), kind=kOutput, calls=%fused_computation.61.clone.1 | convolution fusion | flops 1082130432 | bytes 3442176 | tf_op jit(solution)/shard_map/while/body/eval_jaxpr/dot_general | solution.py:53
  37.6 2.3 %fusion.226 = f32[4096]{0:T(1024)S(1)} fusion(f32[4096]{0:T(1024)S(1)} %broadcast_multiply_fusion.8, bf16[4,4096,128]{2,1,0:T(8,128)(2,1)} %get-tuple-element.694, s32[]{:T(128)S(6)} %copy.206), kind=kLoop, calls=%fused_computation.68.clone.1 | loop fusion | flops 2093056 | bytes 1081348 | tf_op jit(solution)/shard_map/while/body/eval_jaxpr/reduce_sum | solution.py:48
  40.0 4.2 %fusion.227 = bf16[4096,128]{1,0:T(8,128)(2,1)S(1)} fusion(bf16[512,128]{1,0:T(8,128)(2,1)S(1)} %get-tuple-element.697, bf16[128,512]{1,0:T(8,128)(2,1)S(1)} %get-tuple-element.696, f32[128]{0:T(128)S(1)} %get-tuple-element.695, f32[4096]{0:T(1024)S(1)} %add_rsqrt_fusion.8, f32[4096]{0:T(1024)S(1)} %broadcast_multiply_fusion.8, ...), kind=kOutput, calls=%fused_computation.61.clone.1 | convolution fusion | flops 1082130432 | bytes 3442176 | tf_op jit(solution)/shard_map/while/body/eval_jaxpr/dot_general | solution.py:53
  49.7 4.0 %fusion.227 = bf16[4096,128]{1,0:T(8,128)(2,1)S(1)} fusion(bf16[512,128]{1,0:T(8,128)(2,1)S(1)} %get-tuple-element.697, bf16[128,512]{1,0:T(8,128)(2,1)S(1)} %get-tuple-element.696, f32[128]{0:T(128)S(1)} %get-tuple-element.695, f32[4096]{0:T(1024)S(1)} %add_rsqrt_fusion.8, f32[4096]{0:T(1024)S(1)} %broadcast_multiply_fusion.8, ...), kind=kOutput, calls=%fused_computation.61.clone.1 | convolution fusion | flops 1082130432 | bytes 3442176 | tf_op jit(solution)/shard_map/while/body/eval_jaxpr/dot_general | solution.py:53
  60.1 39.0 %while.43 = (s32[]{:T(128)}, f32[4,4096]{1,0:T(4,128)S(1)}, f32[4,4096]{1,0:T(4,128)S(1)}, bf16[4,4096,128]{2,1,0:T(8,128)(2,1)}, f32[128]{0:T(128)S(1)}, /*inde...) while((s32[]{:T(128)}, f32[4,4096]{1,0:T(4,128)S(1)}, ...), condition=%wide.region_15.16_spmd.clone.clone, body=%wide.region_8.15_spmd.clone.clone.sunk | while | flops 1155256576 | bytes 10046353 | solution.py:156
  64.1 4.1 %fusion.216 = bf16[4096,128]{1,0:T(8,128)(2,1)S(1)} fusion(bf16[512,128]{1,0:T(8,128)(2,1)S(1)} %get-tuple-element.733, bf16[128,512]{1,0:T(8,128)(2,1)S(1)} %get-tuple-element.732, f32[128]{0:T(128)S(1)} %get-tuple-element.731, f32[4096]{0:T(1024)S(1)} %add_rsqrt_fusion.7, f32[4096]{0:T(1024)S(1)} %broadcast_multiply_fusion.7, ...), kind=kOutput, calls=%fused_computation.33.clone.1 | convolution fusion | flops 1082130432 | bytes 3442176 | tf_op jit(solution)/shard_map/while/body/eval_jaxpr/dot_general | solution.py:53
  71.4 2.3 %fusion.215 = f32[4096]{0:T(1024)S(1)} fusion(f32[4096]{0:T(1024)S(1)} %broadcast_multiply_fusion.7, bf16[4,4096,128]{2,1,0:T(8,128)(2,1)} %get-tuple-element.730, s32[]{:T(128)S(6)} %copy.215), kind=kLoop, calls=%fused_computation.40.clone.1 | loop fusion | flops 2093056 | bytes 1081348 | tf_op jit(solution)/shard_map/while/body/eval_jaxpr/reduce_sum | solution.py:48
  73.8 4.1 %fusion.216 = bf16[4096,128]{1,0:T(8,128)(2,1)S(1)} fusion(bf16[512,128]{1,0:T(8,128)(2,1)S(1)} %get-tuple-element.733, bf16[128,512]{1,0:T(8,128)(2,1)S(1)} %get-tuple-element.732, f32[128]{0:T(128)S(1)} %get-tuple-element.731, f32[4096]{0:T(1024)S(1)} %add_rsqrt_fusion.7, f32[4096]{0:T(1024)S(1)} %broadcast_multiply_fusion.7, ...), kind=kOutput, calls=%fused_computation.33.clone.1 | convolution fusion | flops 1082130432 | bytes 3442176 | tf_op jit(solution)/shard_map/while/body/eval_jaxpr/dot_general | solution.py:53
  81.1 2.3 %fusion.215 = f32[4096]{0:T(1024)S(1)} fusion(f32[4096]{0:T(1024)S(1)} %broadcast_multiply_fusion.7, bf16[4,4096,128]{2,1,0:T(8,128)(2,1)} %get-tuple-element.730, s32[]{:T(128)S(6)} %copy.215), kind=kLoop, calls=%fused_computation.40.clone.1 | loop fusion | flops 2093056 | bytes 1081348 | tf_op jit(solution)/shard_map/while/body/eval_jaxpr/reduce_sum | solution.py:48
  83.5 4.2 %fusion.216 = bf16[4096,128]{1,0:T(8,128)(2,1)S(1)} fusion(bf16[512,128]{1,0:T(8,128)(2,1)S(1)} %get-tuple-element.733, bf16[128,512]{1,0:T(8,128)(2,1)S(1)} %get-tuple-element.732, f32[128]{0:T(128)S(1)} %get-tuple-element.731, f32[4096]{0:T(1024)S(1)} %add_rsqrt_fusion.7, f32[4096]{0:T(1024)S(1)} %broadcast_multiply_fusion.7, ...), kind=kOutput, calls=%fused_computation.33.clone.1 | convolution fusion | flops 1082130432 | bytes 3442176 | tf_op jit(solution)/shard_map/while/body/eval_jaxpr/dot_general | solution.py:53
  90.9 2.3 %fusion.215 = f32[4096]{0:T(1024)S(1)} fusion(f32[4096]{0:T(1024)S(1)} %broadcast_multiply_fusion.7, bf16[4,4096,128]{2,1,0:T(8,128)(2,1)} %get-tuple-element.730, s32[]{:T(128)S(6)} %copy.215), kind=kLoop, calls=%fused_computation.40.clone.1 | loop fusion | flops 2093056 | bytes 1081348 | tf_op jit(solution)/shard_map/while/body/eval_jaxpr/reduce_sum | solution.py:48
  93.2 4.2 %fusion.216 = bf16[4096,128]{1,0:T(8,128)(2,1)S(1)} fusion(bf16[512,128]{1,0:T(8,128)(2,1)S(1)} %get-tuple-element.733, bf16[128,512]{1,0:T(8,128)(2,1)S(1)} %get-tuple-element.732, f32[128]{0:T(128)S(1)} %get-tuple-element.731, f32[4096]{0:T(1024)S(1)} %add_rsqrt_fusion.7, f32[4096]{0:T(1024)S(1)} %broadcast_multiply_fusion.7, ...), kind=kOutput, calls=%fused_computation.33.clone.1 | convolution fusion | flops 1082130432 | bytes 3442176 | tf_op jit(solution)/shard_map/while/body/eval_jaxpr/dot_general | solution.py:53
  99.9 38.7 %while.42 = (s32[]{:T(128)}, f32[4,4096]{1,0:T(4,128)S(1)}, f32[4,4096]{1,0:T(4,128)S(1)}, bf16[4,4096,128]{2,1,0:T(8,128)(2,1)}, f32[128]{0:T(128)S(1)}, /*inde...) while((s32[]{:T(128)}, f32[4,4096]{1,0:T(4,128)S(1)}, ...), condition=%wide.region_7.8_spmd.clone.clone, body=%wide.region_0.7_spmd.clone.clone.sunk | while | flops 1155256576 | bytes 10046353 | solution.py:156
  101.5 2.3 %fusion.204 = f32[4096]{0:T(1024)S(1)} fusion(f32[4096]{0:T(1024)S(1)} %broadcast_multiply_fusion.6, bf16[4,4096,128]{2,1,0:T(8,128)(2,1)} %get-tuple-element.766, s32[]{:T(128)S(6)} %copy.224), kind=kLoop, calls=%fused_computation.12.clone.1 | loop fusion | flops 2093056 | bytes 1081348 | tf_op jit(solution)/shard_map/while/body/eval_jaxpr/reduce_sum | solution.py:48
  103.8 4.0 %fusion.205 = bf16[4096,128]{1,0:T(8,128)(2,1)S(1)} fusion(bf16[512,128]{1,0:T(8,128)(2,1)S(1)} %get-tuple-element.769, bf16[128,512]{1,0:T(8,128)(2,1)S(1)} %get-tuple-element.768, f32[128]{0:T(128)S(1)} %get-tuple-element.767, f32[4096]{0:T(1024)S(1)} %add_rsqrt_fusion.6, f32[4096]{0:T(1024)S(1)} %broadcast_multiply_fusion.6, ...), kind=kOutput, calls=%fused_computation.5.clone.1 | convolution fusion | flops 1082130432 | bytes 3442176 | tf_op jit(solution)/shard_map/while/body/eval_jaxpr/dot_general | solution.py:53
  111.1 2.3 %fusion.204 = f32[4096]{0:T(1024)S(1)} fusion(f32[4096]{0:T(1024)S(1)} %broadcast_multiply_fusion.6, bf16[4,4096,128]{2,1,0:T(8,128)(2,1)} %get-tuple-element.766, s32[]{:T(128)S(6)} %copy.224), kind=kLoop, calls=%fused_computation.12.clone.1 | loop fusion | flops 2093056 | bytes 1081348 | tf_op jit(solution)/shard_map/while/body/eval_jaxpr/reduce_sum | solution.py:48
  113.4 4.0 %fusion.205 = bf16[4096,128]{1,0:T(8,128)(2,1)S(1)} fusion(bf16[512,128]{1,0:T(8,128)(2,1)S(1)} %get-tuple-element.769, bf16[128,512]{1,0:T(8,128)(2,1)S(1)} %get-tuple-element.768, f32[128]{0:T(128)S(1)} %get-tuple-element.767, f32[4096]{0:T(1024)S(1)} %add_rsqrt_fusion.6, f32[4096]{0:T(1024)S(1)} %broadcast_multiply_fusion.6, ...), kind=kOutput, calls=%fused_computation.5.clone.1 | convolution fusion | flops 1082130432 | bytes 3442176 | tf_op jit(solution)/shard_map/while/body/eval_jaxpr/dot_general | solution.py:53
  123.0 4.0 %fusion.205 = bf16[4096,128]{1,0:T(8,128)(2,1)S(1)} fusion(bf16[512,128]{1,0:T(8,128)(2,1)S(1)} %get-tuple-element.769, bf16[128,512]{1,0:T(8,128)(2,1)S(1)} %get-tuple-element.768, f32[128]{0:T(128)S(1)} %get-tuple-element.767, f32[4096]{0:T(1024)S(1)} %add_rsqrt_fusion.6, f32[4096]{0:T(1024)S(1)} %broadcast_multiply_fusion.6, ...), kind=kOutput, calls=%fused_computation.5.clone.1 | convolution fusion | flops 1082130432 | bytes 3442176 | tf_op jit(solution)/shard_map/while/body/eval_jaxpr/dot_general | solution.py:53
  132.6 4.1 %fusion.205 = bf16[4096,128]{1,0:T(8,128)(2,1)S(1)} fusion(bf16[512,128]{1,0:T(8,128)(2,1)S(1)} %get-tuple-element.769, bf16[128,512]{1,0:T(8,128)(2,1)S(1)} %get-tuple-element.768, f32[128]{0:T(128)S(1)} %get-tuple-element.767, f32[4096]{0:T(1024)S(1)} %add_rsqrt_fusion.6, f32[4096]{0:T(1024)S(1)} %broadcast_multiply_fusion.6, ...), kind=kOutput, calls=%fused_computation.5.clone.1 | convolution fusion | flops 1082130432 | bytes 3442176 | tf_op jit(solution)/shard_map/while/body/eval_jaxpr/dot_general | solution.py:53
  142.5 4.3 %all-to-all-start = ((f32[8,128,129]{1,2,0:T(8,128)}), f32[8,128,129]{1,2,0:T(8,128)S(1)}, u32[]{:S(2)}, u32[]{:S(2)}) async-start(f32[8,128,129]{1,2,0:T(8,128)} %copy.161), calls=%async_computation | async-start | bytes 1114112 | tf_op jit(solution)/shard_map/all_to_all | solution.py:13
  147.5 9.9 %all-to-all-done = f32[8,128,129]{1,2,0:T(8,128)S(1)} async-done(((f32[8,128,129]{1,2,0:T(8,128)}), f32[8,128,129]{1,2,0:T(8,128)S(1)}, u32[]{:S(2)}, u32[]{:S(2)}) %all-to-all-start) | async-done | bytes 528416 | tf_op jit(solution)/shard_map/all_to_all | solution.py:13
  159.0 11.4 %all-to-all-start.2 = ((f32[32,3,16]{2,1,0:T(4,128)}), f32[32,3,16]{2,1,0:T(4,128)S(1)}, u32[]{:S(2)}, u32[]{:S(2)}) async-start(f32[32,3,16]{2,1,0:T(4,128)} %copy.175), calls=%async_computation.2 | async-start | bytes 131072 | tf_op jit(solution)/shard_map/all_to_all | solution.py:201
  170.8 8.7 %all-to-all-done.2 = f32[32,3,16]{2,1,0:T(4,128)S(1)} async-done(((f32[32,3,16]{2,1,0:T(4,128)}), f32[32,3,16]{2,1,0:T(4,128)S(1)}, u32[]{:S(2)}, u32[]{:S(2)}) %all-to-all-start.2) | async-done | bytes 6176 | tf_op jit(solution)/shard_map/all_to_all | solution.py:201
  180.4 4.6 %all-to-all-start.3 = ((f32[32,1,6]{2,1,0:T(1,128)}), f32[32,1,6]{2,1,0:T(1,128)S(1)}, u32[]{:S(2)}, u32[]{:S(2)}) async-start(f32[32,1,6]{2,1,0:T(1,128)} %broadcast_in_dim.60), calls=%async_computation.3 | async-start | bytes 32768 | tf_op jit(solution)/shard_map/all_to_all | solution.py:26
  187.0 6.8 %all-to-all-done.3 = f32[32,1,6]{2,1,0:T(1,128)S(1)} async-done(((f32[32,1,6]{2,1,0:T(1,128)}), f32[32,1,6]{2,1,0:T(1,128)S(1)}, u32[]{:S(2)}, u32[]{:S(2)}) %all-to-all-start.3) | async-done | bytes 800 | tf_op jit(solution)/shard_map/all_to_all | solution.py:26
  193.8 5.0 %all-to-all-start.1 = ((f32[32,3,16,128]{3,2,1,0:T(8,128)}), f32[32,3,16,128]{3,2,1,0:T(8,128)S(1)}, u32[]{:S(2)}, u32[]{:S(2)}) async-start(f32[32,3,16,128]{3,2,1,0:T(8,128)} %copy.164), calls=%async_computation.1 | async-start | bytes 1572864 | tf_op jit(solution)/shard_map/all_to_all | solution.py:200
  199.4 20.0 %all-to-all-done.1 = f32[32,3,16,128]{3,2,1,0:T(8,128)S(1)} async-done(((f32[32,3,16,128]{3,2,1,0:T(8,128)}), f32[32,3,16,128]{3,2,1,0:T(8,128)S(1)}, u32[]{:S(2)}, u32[]{:S(2)}) %all-to-all-start.1) | async-done | bytes 786464 | tf_op jit(solution)/shard_map/all_to_all | solution.py:200
  (186 shorter events, 62.7 us)
Async XLA Ops:
  6.2 9.0 %copy-start.3 = (s32[48]{0:T(128)S(1)}, s32[48]{0:T(128)}, u32[]{:S(2)}) copy-start(s32[48]{0:T(128)} %param.17) | copy-start | bytes 580
  6.2 10.3 %copy-start = (bf16[128,64]{0,1:T(8,128)(2,1)S(1)}, bf16[128,64]{0,1:T(8,128)(2,1)}, u32[]{:S(2)}) copy-start(bf16[128,64]{0,1:T(8,128)(2,1)} %param.22) | copy-start | bytes 49156
  6.3 10.3 %copy-start.1 = (f32[64]{0:T(128)S(1)}, f32[64]{0:T(128)}, u32[]{:S(2)}) copy-start(f32[64]{0:T(128)} %param.23) | copy-start | bytes 772
  6.3 10.3 %copy-start.4 = (bf16[128,512]{1,0:T(8,128)(2,1)S(1)}, bf16[128,512]{1,0:T(8,128)(2,1)}, u32[]{:S(2)}) copy-start(bf16[128,512]{1,0:T(8,128)(2,1)} %param.20) | copy-start | bytes 393220
  6.3 10.3 %copy-start.5 = (bf16[512,128]{1,0:T(8,128)(2,1)S(1)}, bf16[512,128]{1,0:T(8,128)(2,1)}, u32[]{:S(2)}) copy-start(bf16[512,128]{1,0:T(8,128)(2,1)} %param.21) | copy-start | bytes 393220
  6.3 10.3 %copy-start.6 = (f32[128]{0:T(128)S(1)}, f32[128]{0:T(128)}, u32[]{:S(2)}) copy-start(f32[128]{0:T(128)} %param.19) | copy-start | bytes 1540
  16.6 38.8 %copy-start.2 = (s32[48,512]{1,0:T(8,128)S(1)}, s32[48,512]{1,0:T(8,128)}, u32[]{:S(2)}) copy-start(s32[48,512]{1,0:T(8,128)} %param.18) | copy-start | bytes 294916
  142.5 15.0 %all-to-all-start = ((f32[8,128,129]{1,2,0:T(8,128)}), f32[8,128,129]{1,2,0:T(8,128)S(1)}, u32[]{:S(2)}, u32[]{:S(2)}) async-start(f32[8,128,129]{1,2,0:T(8,128)} %copy.161), calls=%async_computation | async-start | bytes 1114112 | tf_op jit(solution)/shard_map/all_to_all | solution.py:13
  159.0 20.5 %all-to-all-start.2 = ((f32[32,3,16]{2,1,0:T(4,128)}), f32[32,3,16]{2,1,0:T(4,128)S(1)}, u32[]{:S(2)}, u32[]{:S(2)}) async-start(f32[32,3,16]{2,1,0:T(4,128)} %copy.175), calls=%async_computation.2 | async-start | bytes 131072 | tf_op jit(solution)/shard_map/all_to_all | solution.py:201
  180.4 13.3 %all-to-all-start.3 = ((f32[32,1,6]{2,1,0:T(1,128)}), f32[32,1,6]{2,1,0:T(1,128)S(1)}, u32[]{:S(2)}, u32[]{:S(2)}) async-start(f32[32,1,6]{2,1,0:T(1,128)} %broadcast_in_dim.60), calls=%async_computation.3 | async-start | bytes 32768 | tf_op jit(solution)/shard_map/all_to_all | solution.py:26
  193.8 25.6 %all-to-all-start.1 = ((f32[32,3,16,128]{3,2,1,0:T(8,128)}), f32[32,3,16,128]{3,2,1,0:T(8,128)S(1)}, u32[]{:S(2)}, u32[]{:S(2)}) async-start(f32[32,3,16,128]{3,2,1,0:T(8,128)} %copy.164), calls=%async_computation.1 | async-start | bytes 1572864 | tf_op jit(solution)/shard_map/all_to_all | solution.py:200
where the time goes:
time: 223 us; the launch traced here: 222 us
  matrix products  58.4 us (26%)
  other arithmetic  57.2 us (26%)
  waiting for transfers between devices  45.4 us (20%)
  starting transfers between devices  25.3 us (11%)
  local copies, waits for them, and re-layouts  23.6 us (11%)
  between operations  10.8 us (5%)
    dot_general x12, matrix products, pair_head(): jnp.dot(hidden, w_out, preferred_element_type=jnp.float32)  48.9 us
    reduce_sum x12, other arithmetic, pair_head(): variance = jnp.mean(centred * centred, axis=-1, keepdims=True)  27.9 us
    all_to_all x1, waiting for transfers between devices, shards(): lax.all_to_all(error_out, 'tile', split_axis=0, concat_axis=0, tiled=True)  20 us
    reduce_sum x12, other arithmetic, pair_head(): row_mean = jnp.mean(values, axis=-1, keepdims=True)  18.9 us
    all_to_all x1, starting transfers between devices, shards(): lax.all_to_all(rows_out, 'tile', split_axis=0, concat_axis=0, tiled=True)  11.4 us
    all_to_all x1, waiting for transfers between devices, in_one_piece(): lax.all_to_all(both, axis, split_axis=split_dim, concat_axis=concat_dim,...  9.94 us
    slice x1, local copies, waits for them, and re-layouts, shards(): pair_tiles[slot].reshape(row_count // block_rows, block_rows, pair_width)  8.93 us
    all_to_all x1, waiting for transfers between devices, shards(): lax.all_to_all(rows_out, 'tile', split_axis=0, concat_axis=0, tiled=True)  8.67 us
  transfers between devices with their start and end apart: 4, of which 4 were waited for; matrix products, arithmetic and copies ran while one was open for 2% of the time, Pallas kernels for 0%

commit v1 on v0

--- a/solution.py
+++ b/solution.py
@@ -1,9 +1,193 @@
+import functools
 import jax
 import jax.numpy as jnp
 from jax import lax
+from jax.experimental import pallas as pl
+from jax.experimental.pallas import tpu as pltpu
 from jax.sharding import PartitionSpec as P
 
 EPS = 1e-05
+LOG2E = 1.4426950408889634
+F32 = jnp.float32
+BF16 = jnp.bfloat16
+
+
+def head_kernel(
+    slots_ref,
+    lengths_ref,
+    x_ref,
+    resolved_ref,
+    gain_ref,
+    w_in_ref,
+    w_out_ref,
+    w_head_ref,
+    bias_ref,
+    err_ref,
+    tm_ref,
+    mix_s,
+    w1_s,
+    w2_s,
+    bias_s,
+    cen_s,
+    tmw_s,
+    tmt_s,
+    *,
+    rows,
+    group,
+):
+    slot = pl.program_id(0)
+    step = pl.program_id(1)
+    side = x_ref.shape[2]
+    chan = x_ref.shape[3]
+    bins = w_head_ref.shape[1]
+    lanes = 128
+
+    @pl.when((slot == 0) & (step == 0))
+    def _():
+        r = lax.broadcasted_iota(jnp.int32, (chan, chan), 0)
+        c = lax.broadcasted_iota(jnp.int32, (chan, chan), 1)
+        mix_s[0:chan, :] = (jnp.where(r == c, 1.0, 0.0) - 1.0 / chan).astype(BF16)
+        mix_s[chan : chan + bins, :] = w_head_ref[...].astype(F32).T.astype(BF16)
+        w1_s[...] = (w_in_ref[...].astype(F32).T * gain_ref[...]).astype(BF16)
+        w2_s[...] = lax.dot_general(
+            w_head_ref[...],
+            w_out_ref[...],
+            (((0,), (1,)), ((), ())),
+            preferred_element_type=F32,
+        ).astype(BF16)
+        bias_s[...] = jnp.broadcast_to(bias_ref[...], (lanes, bins)).T
+        b = lax.broadcasted_iota(jnp.int32, (bins, lanes), 0).astype(F32)
+        cen_s[...] = (b + 0.5) * (31.0 / (bins - 2))
+
+    k = jnp.maximum(slots_ref[slot, 0], 0)
+    length = lengths_ref[k]
+
+    @pl.when(step == 0)
+    def _():
+        size = jnp.full((bins, lanes), jnp.maximum(length, 19).astype(F32) - 15.0, F32)
+        d0 = 1.24 * jnp.exp(jnp.log(size) * (1.0 / 3.0)) - 1.8
+        ratio = cen_s[...] / d0
+        tmw_s[...] = 1.0 / (1.0 + ratio * ratio)
+
+    present = slots_ref[slot, 0] >= 0
+
+    @pl.when(present)
+    def _():
+        cen = jnp.concatenate([cen_s[...]] * group, axis=1)
+        tmw = jnp.concatenate([tmw_s[...]] * group, axis=1)
+        bias = jnp.concatenate([bias_s[...]] * group, axis=1)
+
+        def body(g, carry):
+            row = pl.multiple_of(g * group, group)
+            x = x_ref[0, pl.ds(row, group), :, :].reshape(group * side, chan)
+            first = lax.dot_general(
+                mix_s[...], x, (((1,), (1,)), ((), ())), preferred_element_type=F32
+            )
+            xc = first[:chan]
+            var = jnp.mean(xc * xc, axis=0, keepdims=True)
+            rstd = lax.rsqrt(var + EPS)
+            z = jnp.dot(w1_s[...], xc.astype(BF16), preferred_element_type=F32)
+            h = jnp.maximum(z, 0.0).astype(BF16)
+            y = jnp.dot(w2_s[...], h, preferred_element_type=F32)
+            logits = (first[chan:] + rstd * y + bias) * LOG2E
+            top = jnp.max(logits, axis=0, keepdims=True)
+            p = jnp.exp2(logits - top)
+            s0 = jnp.sum(p, axis=0, keepdims=True)
+            s1 = jnp.sum(p * cen, axis=0, keepdims=True)
+            s2 = jnp.sum(p * tmw, axis=0, keepdims=True)
+            inv = 1.0 / s0
+            expected = s1 * inv
+            term = s2 * inv
+            at = step * rows + row
+            for i in range(group):
+                err_ref[0, pl.ds(at + i, 1), :] = expected[:, i * side : (i + 1) * side]
+                tmt_s[pl.ds(at + i, 1), :] = term[:, i * side : (i + 1) * side]
+            return carry
+
+        lax.fori_loop(0, rows // group, body, 0)
+
+    @pl.when(step == pl.num_programs(1) - 1)
+    def _():
+        @pl.when(present)
+        def _():
+            br = jnp.maximum(slots_ref[slot, 1], 0)
+            bc = jnp.maximum(slots_ref[slot, 2], 0)
+            pos = lax.broadcasted_iota(jnp.int32, (1, side), 1)
+
+            def valid(block):
+                line = resolved_ref[pl.ds(k, 1), :]
+                res = jnp.zeros((1, side), jnp.int32)
+                for b in range(line.shape[1] // side):
+                    res = jnp.where(block == b, line[:, b * side : (b + 1) * side], res)
+                return jnp.where((pos + block * side < length) & (res > 0), 1.0, 0.0)
+
+            row_valid = jnp.broadcast_to(valid(br), (side, side)).T
+            weight = row_valid * valid(bc)
+            err_ref[0] = err_ref[0] * weight
+            tm_ref[0] = jnp.sum((tmt_s[...] * weight).T, axis=0, keepdims=True)
+
+        @pl.when(jnp.logical_not(present))
+        def _():
+            err_ref[...] = jnp.zeros_like(err_ref)
+            tm_ref[...] = jnp.zeros_like(tm_ref)
+
+
+def head(pair_tiles, own_slots, lengths, resolved, ln_gain, w_in, w_out, w_head, head_bias, rows=32, group=4):
+    slots, side, _, chan = pair_tiles.shape
+    hid = w_in.shape[1]
+    bins = w_head.shape[1]
+
+    def whole(*shape):
+        return pl.BlockSpec(shape, lambda s, i, *_: (0,) * len(shape))
+
+    return pl.pallas_call(
+        functools.partial(head_kernel, rows=rows, group=group),
+        grid_spec=pltpu.PrefetchScalarGridSpec(
+            num_scalar_prefetch=2,
+            grid=(slots, side // rows),
+            in_specs=[
+                pl.BlockSpec((1, rows, side, chan), lambda s, i, *_: (s, i, 0, 0)),
+                whole(*resolved.shape),
+                whole(1, chan),
+                whole(chan, hid),
+                whole(hid, chan),
+                whole(chan, bins),
+                whole(1, bins),
+            ],
+            out_specs=[
+                pl.BlockSpec((1, side, side), lambda s, i, *_: (s, 0, 0)),
+                pl.BlockSpec((1, 1, side), lambda s, i, *_: (s, 0, 0)),
+            ],
+            scratch_shapes=[
+                pltpu.VMEM((chan + bins, chan), BF16),
+                pltpu.VMEM((hid, chan), BF16),
+                pltpu.VMEM((bins, hid), BF16),
+                pltpu.VMEM((bins, 128), F32),
+                pltpu.VMEM((bins, 128), F32),
+                pltpu.VMEM((bins, 128), F32),
+                pltpu.VMEM((side, side), F32),
+            ],
+        ),
+        out_shape=[
+            jax.ShapeDtypeStruct((slots, side, side), F32),
+            jax.ShapeDtypeStruct((slots, 1, side), F32),
+        ],
+        compiler_params=pltpu.CompilerParams(
+            dimension_semantics=("arbitrary", "arbitrary"),
+            vmem_limit_bytes=48 * 1024 * 1024,
+        ),
+        name="head",
+    )(
+        own_slots,
+        lengths,
+        pair_tiles,
+        resolved,
+        ln_gain.reshape(1, chan),
+        w_in,
+        w_out,
+        w_head,
+        head_bias.reshape(1, bins),
+    )
 
 
 def in_one_piece(arrays, axis, split_dim, concat_dim, along):
@@ -29,35 +213,6 @@
 def taken_together(array, axis):
     everything = copy_for_each(array, axis)
     return jnp.max(everything, axis=0)
-
-
-def bin_centers(bin_count):
-    bin_step = 31.0 / (bin_count - 2)
-    return (jnp.arange(bin_count, dtype=jnp.float32) + 0.5) * bin_step
-
-
-def d_zero(length):
-    clipped = jnp.maximum(length, 19).astype(jnp.float32)
-    return 1.24 * jnp.cbrt(clipped - 15.0) - 1.8
-
-
-def pair_head(row_block, ln_gain, w_in, w_out, w_head, head_bias, centers, distance):
-    values = row_block.astype(jnp.float32)
-    row_mean = jnp.mean(values, axis=-1, keepdims=True)
-    centred = values - row_mean
-    variance = jnp.mean(centred * centred, axis=-1, keepdims=True)
-    normed = (centred * lax.rsqrt(variance + EPS) * ln_gain).astype(jnp.bfloat16)
-    hidden = jax.nn.relu(jnp.dot(normed, w_in, preferred_element_type=jnp.float32)).astype(
-        jnp.bfloat16
-    )
-    updated = (values + jnp.dot(hidden, w_out, preferred_element_type=jnp.float32)).astype(
-        jnp.bfloat16
-    )
-    logits = jnp.dot(updated, w_head, preferred_element_type=jnp.float32) + head_bias
-    bin_probs = jax.nn.softmax(logits, axis=-1)
-    expected = jnp.sum(bin_probs * centers, axis=-1)
-    tm_term = jnp.sum(bin_probs / (1.0 + (centers / distance) ** 2), axis=-1)
-    return (expected, tm_term)
 
 
 def route_rows(
@@ -125,49 +280,25 @@
     n_cplx = lax.axis_size("cplx")
     row_index = lax.axis_index("tile")
     col_index = lax.axis_index("cplx")
-    slot_count, tile_side, _, pair_width = pair_tiles.shape
+    slot_count, tile_side = pair_tiles.shape[:2]
     complexes, maxres = resolved.shape
     blocks = maxres // tile_side
     cpx_dev = complexes // n_cplx
     rows_each = maxres // n_tile
     parts_per = tile_side // rows_each
-    centers = bin_centers(w_head.shape[1])
     positions = jnp.arange(maxres, dtype=jnp.int32)
     valid_mask = ((positions[None, :] < lengths[:, None]) & (resolved > 0)).astype(jnp.float32)
-    valid_blocks = valid_mask.reshape(complexes, blocks, tile_side)
     layout = tile_map.reshape(n_tile, n_cplx, slot_count, 3)
     own_slots = layout[row_index, col_index]
-    row_count = tile_side * tile_side
-    block_rows = min(4096, row_count)
-    error_tiles = []
-    score_tiles = []
-    owner_list = []
-    for slot in range(slot_count):
-        slot_meta = own_slots[slot]
-        present = slot_meta[0] >= 0
-        complex_id = jnp.maximum(slot_meta[0], 0)
-        block_row = jnp.maximum(slot_meta[1], 0)
-        block_col = jnp.maximum(slot_meta[2], 0)
-        distance = d_zero(lengths[complex_id])
-
-        def head_block(row_block, distance=distance):
-            return pair_head(row_block, ln_gain, w_in, w_out, w_head, head_bias, centers, distance)
-
-        expected, tm_term = lax.map(
-            head_block, pair_tiles[slot].reshape(row_count // block_rows, block_rows, pair_width)
-        )
-        row_valid = valid_blocks[complex_id, block_row]
-        col_valid = valid_blocks[complex_id, block_col]
-        weight = jnp.where(present, row_valid[:, None] * col_valid[None, :], jnp.float32(0.0))
-        error_tiles.append(weight * expected.reshape(tile_side, tile_side))
-        score_tiles.append(weight * tm_term.reshape(tile_side, tile_side))
-        owner_list.append(jnp.where(present, complex_id // cpx_dev, -1))
-    owner_ids = jnp.stack(owner_list)
+    error_tiles, score_rows = head(
+        pair_tiles, own_slots, lengths, resolved, ln_gain, w_in, w_out, w_head, head_bias
+    )
+    score_rows = score_rows[:, 0]
+    owner_ids = jnp.where(own_slots[:, 0] >= 0, own_slots[:, 0] // cpx_dev, -1)
     select = (jnp.arange(n_cplx, dtype=jnp.int32)[:, None] == owner_ids[None, :]).astype(
         jnp.float32
     )
-    error_send = jnp.einsum("os,sij->oij", select, jnp.stack(error_tiles), precision=highest)
-    score_rows = jnp.stack([jnp.sum(score_tile, axis=1) for score_tile in score_tiles])
+    error_send = jnp.einsum("os,sij->oij", select, error_tiles, precision=highest)
     score_send = jnp.einsum("os,si->oi", select, score_rows, precision=highest)
     error_in, rows_in = in_one_piece((error_send, score_send), "cplx", 0, 0, 2)
     complex_all = layout[..., 0]

time: 223 us -> 159 us (0.71)
  Pallas kernels: 0 us -> 68.6 us
  other arithmetic: 57.2 us -> 2.18 us
  matrix products: 58.4 us -> 3.42 us
  local copies, waits for them, and re-layouts: 23.6 us -> 12.4 us
  between operations: 10.8 us -> 0.86 us
    pallas_call x0 -> x1, Pallas kernels: none -> 68.6 us  [head(): pl.pallas_call(functools.partial(head_kernel, rows=rows, group=group), gr...]
    dot_general x25 -> x1, matrix products: 55.5 us -> 0.56 us  [shards(): jnp.einsum('os,sij->oij', select, error_tiles, precision=highest)]
    reduce_sum x50 -> x0, other arithmetic: 54.4 us -> none  [the longest x12 27.9 us: pair_head(): variance = jnp.mean(centred * centred, axis=-1, keepdims=True)]
    slice x2 -> x0, local copies, waits for them, and re-layouts: 9.61 us -> none  [the longest x1 8.93 us: shards(): pair_tiles[slot].reshape(row_count // block_rows, block_rows, pair_width)]
    dynamic_update_slice x24 -> x0, local copies, waits for them, and re-layouts: 5.96 us -> none  [shards(): lax.map(head_block, pair_tiles[slot].reshape(row_count // block_rows, blo...]
    unnamed x14 -> x17, local copies, waits for them, and re-layouts: 0.04 us -> 5.5 us
where the time goes in v1:
time: 159 us; the launch traced here: 158 us
  Pallas kernels  68.6 us (43%)
  waiting for transfers between devices  45.1 us (28%)
  starting transfers between devices  25 us (16%)
  local copies, waits for them, and re-layouts  12.4 us (8%)
  matrix products  3.42 us (2%)
  other arithmetic  2.18 us (1%)
    pallas_call x1, Pallas kernels, head(): pl.pallas_call(functools.partial(head_kernel, rows=rows, group=group), gr...  68.6 us
    all_to_all x1, waiting for transfers between devices, shards(): lax.all_to_all(error_out, 'tile', split_axis=0, concat_axis=0, tiled=True)  20 us
    all_to_all x1, starting transfers between devices, shards(): lax.all_to_all(rows_out, 'tile', split_axis=0, concat_axis=0, tiled=True)  11.7 us
    all_to_all x1, waiting for transfers between devices, in_one_piece(): lax.all_to_all(both, axis, split_axis=split_dim, concat_axis=concat_dim,...  9.73 us
    all_to_all x1, waiting for transfers between devices, shards(): lax.all_to_all(rows_out, 'tile', split_axis=0, concat_axis=0, tiled=True)  8.67 us
    all_to_all x1, waiting for transfers between devices, copy_for_each(): return lax.all_to_all(copies, axis, split_axis=0, concat_axis=0, tiled=True)  6.75 us
    unnamed x17, local copies, waits for them, and re-layouts  5.5 us
    all_to_all x1, starting transfers between devices, shards(): lax.all_to_all(error_out, 'tile', split_axis=0, concat_axis=0, tiled=True)  4.97 us
  transfers between devices with their start and end apart: 4, of which 4 were waited for; matrix products, arithmetic and copies ran while one was open for 2% of the time, Pallas kernels for 0%

profile of v1, /device:TPU:32, one launch (start us, length us, event | category | flops | bytes accessed | tf_op | source)
XLA Modules:
  0.0 157.7 jit_solution(13743023310878876797)
XLA Ops:
  0.7 1.0 reshape.125
  2.1 0.8 copy.191.w_head_ref
  2.9 0.9 copy-done
  3.8 0.9 copy-done.2
  4.7 0.9 copy-done.3
  5.6 0.7 copy-done.4
  6.3 0.7 copy-done.6
  7.0 0.7 copy-done.7
  7.6 68.6 %head.1 = (f32[3,128,128]{2,1,0:T(8,128)S(1)}, f32[3,1,128]{2,1,0:T(1,128)S(1)}) custom-call(s32[3,3]{1,0:T(4,128)S(1)} %bitcast.85, s32[48]{0:T(128)S(1)} %copy-done.4, bf16[3,128,128,128]{3,2,1,0:T(8,128)(2,1)} %x_ref.1, s32[48,512]{1,0:T(8,128)S(1)} %copy-done, f32[1,128]{1,0:T(1,128)S(1)} %bitcast.86, bf16[128,512]{1,0:T(8,128)(2,1)S(1)} %copy-done.2, ...), custom_call_target="tpu_custom_call" | custom-call | tf_op jit(solution)/shard_map/head/pallas_call | solution.py:143
  76.2 0.3 convolution_bitcast_fusion.3
  76.5 0.3 copy.193
  76.8 0.6 fusion.3
  77.4 1.2 copy.194
  78.6 3.7 %all-to-all-start = ((f32[8,128,129]{1,2,0:T(8,128)}), f32[8,128,129]{1,2,0:T(8,128)S(1)}, u32[]{:S(2)}, u32[]{:S(2)}) async-start(f32[8,128,129]{1,2,0:T(8,128)} %copy.194), calls=%async_computation | async-start | bytes 1114112 | tf_op jit(solution)/shard_map/all_to_all | solution.py:197
  83.3 9.7 %all-to-all-done = f32[8,128,129]{1,2,0:T(8,128)S(1)} async-done(((f32[8,128,129]{1,2,0:T(8,128)}), f32[8,128,129]{1,2,0:T(8,128)S(1)}, u32[]{:S(2)}, u32[]{:S(2)}) %all-to-all-start) | async-done | bytes 528416 | tf_op jit(solution)/shard_map/all_to_all | solution.py:197
  93.6 0.2 convolution_bitcast_fusion.2
  93.9 0.7 copy.208
  94.6 11.7 %all-to-all-start.2 = ((f32[32,3,16]{2,1,0:T(4,128)}), f32[32,3,16]{2,1,0:T(4,128)S(1)}, u32[]{:S(2)}, u32[]{:S(2)}) async-start(f32[32,3,16]{2,1,0:T(4,128)} %copy.208), calls=%async_computation.2 | async-start | bytes 131072 | tf_op jit(solution)/shard_map/all_to_all | solution.py:332
  106.2 0.4 fusion.38
  106.7 8.7 %all-to-all-done.2 = f32[32,3,16]{2,1,0:T(4,128)S(1)} async-done(((f32[32,3,16]{2,1,0:T(4,128)}), f32[32,3,16]{2,1,0:T(4,128)S(1)}, u32[]{:S(2)}, u32[]{:S(2)}) %all-to-all-start.2) | async-done | bytes 6176 | tf_op jit(solution)/shard_map/all_to_all | solution.py:332
  115.3 0.3 fusion.1
  115.7 0.6 broadcast_in_dim.9
  116.3 4.6 %all-to-all-start.3 = ((f32[32,1,6]{2,1,0:T(1,128)}), f32[32,1,6]{2,1,0:T(1,128)S(1)}, u32[]{:S(2)}, u32[]{:S(2)}) async-start(f32[32,1,6]{2,1,0:T(1,128)} %broadcast_in_dim.9), calls=%async_computation.3 | async-start | bytes 32768 | tf_op jit(solution)/shard_map/all_to_all | solution.py:210
  120.9 0.6 convolution_bitcast_fusion
  121.5 1.3 copy.197
  122.9 6.7 %all-to-all-done.3 = f32[32,1,6]{2,1,0:T(1,128)S(1)} async-done(((f32[32,1,6]{2,1,0:T(1,128)}), f32[32,1,6]{2,1,0:T(1,128)S(1)}, u32[]{:S(2)}, u32[]{:S(2)}) %all-to-all-start.3) | async-done | bytes 800 | tf_op jit(solution)/shard_map/all_to_all | solution.py:210
  129.6 5.0 %all-to-all-start.1 = ((f32[32,3,16,128]{3,2,1,0:T(8,128)}), f32[32,3,16,128]{3,2,1,0:T(8,128)S(1)}, u32[]{:S(2)}, u32[]{:S(2)}) async-start(f32[32,3,16,128]{3,2,1,0:T(8,128)} %copy.197), calls=%async_computation.1 | async-start | bytes 1572864 | tf_op jit(solution)/shard_map/all_to_all | solution.py:331
  134.7 0.6 reduce_max.19
  135.3 20.0 %all-to-all-done.1 = f32[32,3,16,128]{3,2,1,0:T(8,128)S(1)} async-done(((f32[32,3,16,128]{3,2,1,0:T(8,128)}), f32[32,3,16,128]{3,2,1,0:T(8,128)S(1)}, u32[]{:S(2)}, u32[]{:S(2)}) %all-to-all-start.1) | async-done | bytes 786464 | tf_op jit(solution)/shard_map/all_to_all | solution.py:331
  155.2 0.8 fusion.60
  156.2 0.8 reshape.129
  157.0 0.7 fusion.40
  (38 shorter events, 2.1 us)
Async XLA Ops:
  0.6 81.9 %copy-start.5 = (s32[48]{0:T(128)S(1)}, s32[48]{0:T(128)}, u32[]{:S(2)}) copy-start(s32[48]{0:T(128)} %lengths_ref.1) | copy-start | bytes 580
  0.6 81.9 %copy-start.1 = (s32[48,512]{1,0:T(8,128)S(1)}, s32[48,512]{1,0:T(8,128)}, u32[]{:S(2)}) copy-start(s32[48,512]{1,0:T(8,128)} %resolved_ref.1) | copy-start | bytes 294916
  2.9 0.9 copy-start
  3.8 0.9 copy-start.2
  4.7 0.9 copy-start.3
  5.6 0.7 copy-start.4
  6.3 0.7 copy-start.6
  6.9 0.7 copy-start.7
  78.6 14.4 %all-to-all-start = ((f32[8,128,129]{1,2,0:T(8,128)}), f32[8,128,129]{1,2,0:T(8,128)S(1)}, u32[]{:S(2)}, u32[]{:S(2)}) async-start(f32[8,128,129]{1,2,0:T(8,128)} %copy.194), calls=%async_computation | async-start | bytes 1114112 | tf_op jit(solution)/shard_map/all_to_all | solution.py:197
  94.6 20.8 %all-to-all-start.2 = ((f32[32,3,16]{2,1,0:T(4,128)}), f32[32,3,16]{2,1,0:T(4,128)S(1)}, u32[]{:S(2)}, u32[]{:S(2)}) async-start(f32[32,3,16]{2,1,0:T(4,128)} %copy.208), calls=%async_computation.2 | async-start | bytes 131072 | tf_op jit(solution)/shard_map/all_to_all | solution.py:332
  116.3 13.3 %all-to-all-start.3 = ((f32[32,1,6]{2,1,0:T(1,128)}), f32[32,1,6]{2,1,0:T(1,128)S(1)}, u32[]{:S(2)}, u32[]{:S(2)}) async-start(f32[32,1,6]{2,1,0:T(1,128)} %broadcast_in_dim.9), calls=%async_computation.3 | async-start | bytes 32768 | tf_op jit(solution)/shard_map/all_to_all | solution.py:210
  129.6 25.6 %all-to-all-start.1 = ((f32[32,3,16,128]{3,2,1,0:T(8,128)}), f32[32,3,16,128]{3,2,1,0:T(8,128)S(1)}, u32[]{:S(2)}, u32[]{:S(2)}) async-start(f32[32,3,16,128]{3,2,1,0:T(8,128)} %copy.197), calls=%async_computation.1 | async-start | bytes 1572864 | tf_op jit(solution)/shard_map/all_to_all | solution.py:331

commit v2 on v0

v2 whole, which is shorter than its diff:
```python
import functools
import jax
import jax.numpy as jnp
from jax import lax
from jax.experimental import pallas as pl
from jax.experimental.pallas import tpu as pltpu
from jax.sharding import PartitionSpec as P

EPS = 1e-05
LOG2E = 1.4426950408889634
F32 = jnp.float32
BF16 = jnp.bfloat16
MESH = pl.DeviceIdType.MESH
GROUP = 4


def fused_kernel(
    table_ref,
    lengths_ref,
    x_ref,
    resolved_ref,
    gain_ref,
    w_in_ref,
    w_out_ref,
    w_head_ref,
    bias_ref,
    map_ref,
    res_ref,
    best_ref,
    mix_s,
    w1_s,
    w2_s,
    bias_s,
    cen_s,
    tmw_s,
    weight_s,
    x_s,
    err_s,
    tm_s,
    send_s,
    sendt_s,
    recv_s,
    recvt_s,
    ysend_s,
    ysendt_s,
    yrecv_s,
    yrecvt_s,
    top_s,
    topz_s,
    topy_s,
    x_sem,
    send_sem,
    sendt_sem,
    recv_sem,
    recvt_sem,
    ysend_sem,
    yrecv_sem,
    yrecvt_sem,
    topsend_sem,
    topz_sem,
    topy_sem,
    *,
    blocks,
    parts,
    n_cplx,
):
    slots, side, _, chan = x_ref.shape
    bins = w_head_ref.shape[1]
    lanes = 128
    rows = side // parts
    cpx_dev = map_ref.shape[0]
    cells = cpx_dev * blocks
    tile = lax.axis_index("tile")
    mine = lax.axis_index("cplx")
    by = tile // parts
    bz = lax.rem(tile, parts)

    def x_copy(s, j):
        p = lax.rem(bz + parts - 1 - s, parts)
        at = lax.rem(s, 2)
        return pltpu.make_async_copy(
            x_ref.at[j, pl.ds(p * rows, rows)],
            x_s.at[at, pl.ds(j * rows, rows)],
            x_sem.at[at, j],
        )

    for j in range(slots):
        x_copy(0, j).start()

    barrier = pltpu.get_barrier_semaphore()
    plane = parts * n_cplx

    def greet(d, carry):
        other = lax.rem(bz * n_cplx + mine + d, plane)
        pl.semaphore_signal(
            barrier,
            inc=1,
            device_id=(by * parts + other // n_cplx, lax.rem(other, n_cplx)),
            device_id_type=MESH,
        )
        return carry

    lax.fori_loop(1, plane, greet, 0)
    for d in range(1, blocks):
        pl.semaphore_signal(
            barrier,
            inc=1,
            device_id=(lax.rem(by + d, blocks) * parts + bz, mine),
            device_id_type=MESH,
        )

    r = lax.broadcasted_iota(jnp.int32, (chan, chan), 0)
    c = lax.broadcasted_iota(jnp.int32, (chan, chan), 1)
    mix_s[0:chan, :] = (jnp.where(r == c, 1.0, 0.0) - 1.0 / chan).astype(BF16)
    mix_s[chan : chan + bins, :] = w_head_ref[...].astype(F32).T.astype(BF16)
    w1_s[...] = (w_in_ref[...].astype(F32).T * gain_ref[...]).astype(BF16)
    w2_s[...] = lax.dot_general(
        w_head_ref[...], w_out_ref[...], (((0,), (1,)), ((), ())), preferred_element_type=F32
    ).astype(BF16)
    bias_s[...] = jnp.broadcast_to(bias_ref[...], (lanes, bins)).T
    b = lax.broadcasted_iota(jnp.int32, (bins, lanes), 0).astype(F32)
    cen_s[...] = (b + 0.5) * (31.0 / (bins - 2))
    pos = lax.broadcasted_iota(jnp.int32, (1, side), 1)

    def valid(k, length, block):
        line = resolved_ref[pl.ds(k, 1), :]
        part = jnp.zeros((1, side), jnp.int32)
        for q in range(blocks):
            part = jnp.where(block == q, line[:, q * side : (q + 1) * side], part)
        return jnp.where((pos + block * side < length) & (part > 0), 1.0, 0.0)

    owners = []
    for j in range(slots):
        found = table_ref[3 * j]
        k = jnp.maximum(found, 0)
        length = lengths_ref[k]
        size = jnp.full((bins, lanes), jnp.maximum(length, 19).astype(F32) - 15.0, F32)
        d0 = 1.24 * jnp.exp(jnp.log(size) * (1.0 / 3.0)) - 1.8
        ratio = cen_s[...] / d0
        tmw_s[j] = 1.0 / (1.0 + ratio * ratio)
        row_valid = valid(k, length, jnp.maximum(table_ref[3 * j + 1], 0))
        col_valid = valid(k, length, jnp.maximum(table_ref[3 * j + 2], 0))
        col_valid = jnp.where(found >= 0, col_valid, 0.0)
        weight_s[j] = jnp.broadcast_to(row_valid, (side, side)).T * col_valid
        owners.append(jnp.where(found >= 0, k // cpx_dev, -1))

    per_slot = rows // GROUP
    tm_s[...] = jnp.zeros_like(tm_s)

    def err_copy(s, d):
        p = lax.rem(bz + parts - 1 - s, parts)
        o = lax.rem(mine + d, n_cplx)
        return pltpu.make_async_remote_copy(
            src_ref=send_s.at[s, o],
            dst_ref=recv_s.at[bz * n_cplx + mine],
            send_sem=send_sem.at[s],
            recv_sem=recv_sem.at[bz],
            device_id=(by * parts + p, o),
            device_id_type=MESH,
        )

    def tm_copy(s, d):
        p = lax.rem(bz + parts - 1 - s, parts)
        o = lax.rem(mine + d, n_cplx)
        return pltpu.make_async_remote_copy(
            src_ref=sendt_s.at[s],
            dst_ref=recvt_s.at[bz * n_cplx + mine],
            send_sem=sendt_sem.at[s],
            recv_sem=recvt_sem.at[bz],
            device_id=(by * parts + p, o),
            device_id_type=MESH,
        )

    def stage(s, carry):
        at = lax.rem(s, 2)

        @pl.when(s < parts - 1)
        def _():
            for j in range(slots):
                x_copy(s + 1, j).start()

        for j in range(slots):
            x_copy(s, j).wait()

        def body(it, inner):
            row = pl.multiple_of(it * GROUP, GROUP)
            slot = it // per_slot
            x = x_s[at, pl.ds(row, GROUP), :, :].reshape(GROUP * side, chan)
            cen = jnp.concatenate([cen_s[...]] * GROUP, axis=1)
            tmw = jnp.concatenate([tmw_s[slot]] * GROUP, axis=1)
            bias = jnp.concatenate([bias_s[...]] * GROUP, axis=1)
            first = lax.dot_general(
                mix_s[...], x, (((1,), (1,)), ((), ())), preferred_element_type=F32
            )
            xc = first[:chan]
            var = jnp.mean(xc * xc, axis=0, keepdims=True)
            rstd = lax.rsqrt(var + EPS)
            z = jnp.dot(w1_s[...], xc.astype(BF16), preferred_element_type=F32)
            h = jnp.maximum(z, 0.0).astype(BF16)
            y = jnp.dot(w2_s[...], h, preferred_element_type=F32)
            logits = (first[chan:] + rstd * y + bias) * LOG2E
            top = jnp.max(logits, axis=0, keepdims=True)
            e = jnp.exp2(logits - top)
            s0 = jnp.sum(e, axis=0, keepdims=True)
            s1 = jnp.sum(e * cen, axis=0, keepdims=True)
            s2 = jnp.sum(e * tmw, axis=0, keepdims=True)
            inv = 1.0 / s0
            expected = s1 * inv
            term = s2 * inv
            for i in range(GROUP):
                err_s[pl.ds(row + i, 1), :] = expected[:, i * side : (i + 1) * side]
                tm_s[pl.ds(row + i, 1), :] = term[:, i * side : (i + 1) * side]
            return inner

        lax.fori_loop(0, slots * per_slot, body, 0)

        p = lax.rem(bz + parts - 1 - s, parts)
        start = pl.multiple_of(p * rows, rows)
        errs = []
        for j in range(slots):
            weight = weight_s[j, pl.ds(start, rows), :]
            errs.append(err_s[j * rows : (j + 1) * rows, :] * weight)
            tm_s[j * rows : (j + 1) * rows, :] = tm_s[j * rows : (j + 1) * rows, :] * weight
        sendt_s[s] = jnp.sum(tm_s[...].T, axis=0, keepdims=True)
        for o in range(n_cplx):
            piece = jnp.zeros_like(errs[0])
            for j in range(slots):
                piece = jnp.where(owners[j] == o, errs[j], piece)
            send_s[s, o] = piece

        @pl.when(s == 0)
        def _():
            pl.semaphore_wait(barrier, plane - 1 + blocks - 1)

        for d in range(1, n_cplx):
            err_copy(s, d).start()
            tm_copy(s, d).start()

        @pl.when(s < parts - 1)
        def _():
            err_copy(s, 0).start()
            tm_copy(s, 0).start()

        @pl.when(s == parts - 1)
        def _():
            recv_s[bz * n_cplx + mine] = send_s[s, mine]
            recvt_s[bz * n_cplx + mine] = sendt_s[s]

        return carry

    lax.fori_loop(0, parts, stage, 0)

    def await_err(zs, count):
        spot = recv_s.at[pl.ds(zs * n_cplx, count)]
        pltpu.make_async_copy(spot, spot, recv_sem.at[zs]).wait()
        spot = recvt_s.at[pl.ds(zs * n_cplx, count)]
        pltpu.make_async_copy(spot, spot, recvt_sem.at[zs]).wait()

    def arrive(d, carry):
        await_err(lax.rem(bz + d, parts), n_cplx)
        return carry

    lax.fori_loop(1, parts, arrive, 0)
    await_err(bz, n_cplx - 1)

    base = 3 * slots
    per_tile = n_cplx * slots

    def pick(at):
        n = jnp.maximum(table_ref[base + at] - 1, 0)
        t = n // per_tile
        o = lax.rem(n, per_tile) // slots
        j = lax.rem(n, slots)
        return t // parts, lax.rem(t, parts) * n_cplx + o, j

    def gather(i, carry):
        yy = i // cells
        cell = lax.rem(i, cells)
        _, src, j = pick(i)
        ysend_s[yy, cell] = recv_s[src]
        line = recvt_s[src]
        short = line[:, 0:rows]
        for q in range(1, slots):
            short = jnp.where(j == q, line[:, q * rows : (q + 1) * rows], short)
        ysendt_s[yy, cell, :, 0:rows] = short
        return carry

    lax.fori_loop(0, blocks * cells, gather, 0)

    def y_copy(d, small):
        to = lax.rem(by + d, blocks)
        src, dst, sem = (
            (ysendt_s, yrecvt_s, yrecvt_sem) if small else (ysend_s, yrecv_s, yrecv_sem)
        )
        return pltpu.make_async_remote_copy(
            src_ref=src.at[to],
            dst_ref=dst.at[by],
            send_sem=ysend_sem.at[int(small), d],
            recv_sem=sem.at[by],
            device_id=(to * parts + bz, mine),
            device_id_type=MESH,
        )

    order = sorted(range(1, blocks), key=lambda d: -min(d, blocks - d))
    for d in order:
        y_copy(d, True).start()
        y_copy(d, False).start()
    yrecv_s[by] = ysend_s[by]
    yrecvt_s[by] = ysendt_s[by]

    def y_wait(ref, sem, ys):
        pltpu.make_async_copy(ref.at[ys], ref.at[ys], sem.at[ys]).wait()

    for d in range(1, blocks):
        y_wait(yrecvt_s, yrecvt_sem, lax.rem(by + d, blocks))

    denoms = []
    best = []
    for m in range(cpx_dev):
        k = mine * cpx_dev + m
        length = lengths_ref[k]
        line = resolved_ref[pl.ds(k, 1), :]
        where = lax.broadcasted_iota(jnp.int32, line.shape, 1)
        total = jnp.sum(
            jnp.where((where < length) & (line > 0), 1.0, 0.0), axis=1, keepdims=True
        )
        own = pltpu.roll(valid(k, length, by), lax.rem(side - bz * rows, side), 1)[:, 0:rows]
        denom = jnp.maximum(own * total, 1.0)
        denoms.append(denom)
        acc = jnp.zeros((1, rows), F32)
        for q in range(blocks):
            at = by * cells + m * blocks + q
            ys, _, _ = pick(at)
            there = table_ref[base + at] > 0
            acc = acc + jnp.where(there, yrecvt_s[ys, m * blocks + q][:, 0:rows], 0.0)
        best.append(jnp.max(acc / denom, axis=1, keepdims=True))
    for m in range(cpx_dev):
        top_s[0, m] = jnp.broadcast_to(best[m], (1, lanes))

    def top_copy(axis, d):
        if axis == 0:
            device, dst, sem, spot = by * parts + lax.rem(bz + d, parts), topz_s, topz_sem, bz
        else:
            device, dst, sem, spot = lax.rem(by + d, blocks) * parts + bz, topy_s, topy_sem, by
        return pltpu.make_async_remote_copy(
            src_ref=top_s.at[axis],
            dst_ref=dst.at[spot],
            send_sem=topsend_sem.at[axis, d],
            recv_sem=sem.at[spot],
            device_id=(device, mine),
            device_id_type=MESH,
        )

    for d in range(1, parts):
        top_copy(0, d).start()

    for d in range(1, blocks):
        y_wait(yrecv_s, yrecv_sem, lax.rem(by + d, blocks))
    for m in range(cpx_dev):
        total = jnp.zeros((rows, side), F32)
        for q in range(blocks):
            at = by * cells + m * blocks + q
            ys, _, _ = pick(at)
            there = table_ref[base + at] > 0
            piece = jnp.where(there, yrecv_s[ys, m * blocks + q], 0.0)
            map_ref[m, :, q * side : (q + 1) * side] = piece
            total = total + piece
        res_ref[pl.ds(m, 1), :] = jnp.sum(total.T, axis=0, keepdims=True) / denoms[m]

    best = top_s[0]
    for d in range(1, parts):
        zs = lax.rem(bz + d, parts)
        y_wait(topz_s, topz_sem, zs)
        best = jnp.maximum(best, topz_s[zs])
    top_s[1] = best
    for d in range(1, blocks):
        top_copy(1, d).start()
    for d in range(1, blocks):
        ys = lax.rem(by + d, blocks)
        y_wait(topy_s, topy_sem, ys)
        best = jnp.maximum(best, topy_s[ys])
    best_ref[...] = best

    def drain(s, count):
        spot = send_s.at[s, pl.ds(0, count)]
        pltpu.make_async_copy(spot, spot, send_sem.at[s]).wait()
        spot = recvt_s.at[pl.ds(0, count)]
        pltpu.make_async_copy(spot, spot, sendt_sem.at[s]).wait()

    def drain_all(s, carry):
        drain(s, n_cplx)
        return carry

    lax.fori_loop(0, parts - 1, drain_all, 0)
    drain(parts - 1, n_cplx - 1)
    for d in range(1, blocks):
        y_copy(d, True).wait_send()
        y_copy(d, False).wait_send()
    for d in range(1, parts):
        top_copy(0, d).wait_send()
    for d in range(1, blocks):
        top_copy(1, d).wait_send()


def shards(pair_tiles, tile_map, lengths, resolved, ln_gain, w_in, w_out, w_head, head_bias):
    n_tile = lax.axis_size("tile")
    n_cplx = lax.axis_size("cplx")
    slots, side, _, chan = pair_tiles.shape
    hid = w_in.shape[1]
    bins = w_head.shape[1]
    complexes, maxres = resolved.shape
    blocks = maxres // side
    cpx_dev = complexes // n_cplx
    rows = maxres // n_tile
    parts = side // rows
    cells = cpx_dev * blocks
    mine = lax.axis_index("cplx")
    device = lax.axis_index("tile") * n_cplx + mine
    own = lax.dynamic_slice_in_dim(tile_map, device * slots, slots).reshape(3 * slots)
    member = tile_map[:, 0] - mine * cpx_dev
    cell = (tile_map[:, 1] * cpx_dev + member) * blocks + tile_map[:, 2]
    cell = jnp.where((tile_map[:, 0] >= 0) & (member >= 0) & (member < cpx_dev), cell, -1)
    number = jnp.arange(tile_map.shape[0], dtype=jnp.int32) + 1
    want = jnp.arange(blocks * cells, dtype=jnp.int32)
    inverse = jnp.sum(jnp.where(cell[None, :] == want[:, None], number[None, :], 0), axis=1)
    table = jnp.concatenate([own, inverse])
    vmem = pl.BlockSpec(memory_space=pltpu.VMEM)
    smem = pl.BlockSpec(memory_space=pltpu.SMEM)
    dma = pltpu.SemaphoreType.DMA
    error_map, residue, best = pl.pallas_call(
        functools.partial(fused_kernel, blocks=blocks, parts=parts, n_cplx=n_cplx),
        in_specs=[smem, smem, pl.BlockSpec(memory_space=pl.ANY)] + [vmem] * 6,
        out_specs=[vmem] * 3,
        out_shape=[
            jax.ShapeDtypeStruct((cpx_dev, rows, maxres), F32),
            jax.ShapeDtypeStruct((cpx_dev, rows), F32),
            jax.ShapeDtypeStruct((cpx_dev, 1, 128), F32),
        ],
        scratch_shapes=[
            pltpu.VMEM((chan + bins, chan), BF16),
            pltpu.VMEM((hid, chan), BF16),
            pltpu.VMEM((bins, hid), BF16),
            pltpu.VMEM((bins, 128), F32),
            pltpu.VMEM((bins, 128), F32),
            pltpu.VMEM((slots, bins, 128), F32),
            pltpu.VMEM((slots, side, side), F32),
            pltpu.VMEM((2, slots * rows, side, chan), BF16),
            pltpu.VMEM((slots * rows, side), F32),
            pltpu.VMEM((128, side), F32),
            pltpu.VMEM((parts, n_cplx, rows, side), F32),
            pltpu.VMEM((parts, 1, 128), F32),
            pltpu.VMEM((parts * n_cplx, rows, side), F32),
            pltpu.VMEM((parts * n_cplx, 1, 128), F32),
            pltpu.VMEM((blocks, cells, rows, side), F32),
            pltpu.VMEM((blocks, cells, 1, 128), F32),
            pltpu.VMEM((blocks, cells, rows, side), F32),
            pltpu.VMEM((blocks, cells, 1, 128), F32),
            pltpu.VMEM((2, cpx_dev, 1, 128), F32),
            pltpu.VMEM((parts, cpx_dev, 1, 128), F32),
            pltpu.VMEM((blocks, cpx_dev, 1, 128), F32),
            dma((2, slots)),
            dma((parts,)),
            dma((parts,)),
            dma((parts,)),
            dma((parts,)),
            dma((2, blocks)),
            dma((blocks,)),
            dma((blocks,)),
            dma((2, max(parts, blocks))),
            dma((parts,)),
            dma((blocks,)),
        ],
        compiler_params=pltpu.CompilerParams(
            collective_id=0, has_side_effects=True, vmem_limit_bytes=60 * 1024 * 1024
        ),
        name="fused",
    )(
        table,
        lengths,
        pair_tiles,
        resolved,
        ln_gain.reshape(1, chan),
        w_in,
        w_out,
        w_head,
        head_bias.reshape(1, bins),
    )
    return error_map, residue, best[:, 0, 0]


def solution(mesh):
    placed = (P(("tile", "cplx"), None, None, None), P(), P(), P(), P(), P(), P(), P(), P())
    return jax.shard_map(
        shards,
        mesh=mesh,
        in_specs=placed,
        out_specs=(P("cplx", "tile", None), P("cplx", "tile"), P("cplx")),
        check_vma=False,
    )
```

time: 223 us -> 126 us (0.57)
  Pallas kernels: 0 us -> 117 us
  matrix products: 58.4 us -> 0 us
  other arithmetic: 57.2 us -> 1.56 us
  waiting for transfers between devices: 45.4 us -> 0 us
  starting transfers between devices: 25.3 us -> 0 us
  local copies, waits for them, and re-layouts: 23.6 us -> 6.57 us
  between operations: 10.8 us -> 0.66 us
    pallas_call x0 -> x1, Pallas kernels: none -> 117 us  [shards(): pl.pallas_call(functools.partial(fused_kernel, blocks=blocks, parts=parts...]
    dot_general x32 -> x0, matrix products: 58.4 us -> none  [the longest x12 48.9 us: pair_head(): jnp.dot(hidden, w_out, preferred_element_type=jnp.float32)]
    reduce_sum x52 -> x1, other arithmetic: 54.7 us -> 0.12 us  [shards(): jnp.sum(jnp.where(cell[None, :] == want[:, None], number[None, :], 0), ax...]
    all_to_all x4 -> x0, waiting for transfers between devices: 45.4 us -> none  [the longest x1 20 us: shards(): lax.all_to_all(error_out, 'tile', split_axis=0, concat_axis=0, tiled=True)]
    all_to_all x4 -> x0, starting transfers between devices: 25.3 us -> none  [the longest x1 11.4 us: shards(): lax.all_to_all(rows_out, 'tile', split_axis=0, concat_axis=0, tiled=True)]
    slice x3 -> x1, local copies, waits for them, and re-layouts: 9.62 us -> 1.31 us  [shards(): return (error_map, residue, best[:, 0, 0])]
    dynamic_update_slice x24 -> x0, local copies, waits for them, and re-layouts: 5.96 us -> none  [shards(): lax.map(head_block, pair_tiles[slot].reshape(row_count // block_rows, blo...]
    unnamed x14 -> x3, local copies, waits for them, and re-layouts: 0.04 us -> 4.31 us
  transfers between devices with their start and end apart: 4 -> 0, of which waited for: 4 -> 0; matrix products, arithmetic and copies ran while one was open for 2% -> 0% of each run, Pallas kernels for 0% -> 0%
where the time goes in v2:
time: 126 us
  Pallas kernels  117 us (93%)
  local copies, waits for them, and re-layouts  6.57 us (5%)
  other arithmetic  1.56 us (1%)
    pallas_call x1, Pallas kernels, shards(): pl.pallas_call(functools.partial(fused_kernel, blocks=blocks, parts=parts...  117 us
    unnamed x3, local copies, waits for them, and re-layouts  4.31 us

profile of v2, /device:TPU:32, one launch (start us, length us, event | category | flops | bytes accessed | tf_op | source)
XLA Modules:
  0.0 125.7 jit_solution(6794302764598977845)
XLA Ops:
  0.6 0.8 constant_dynamic-slice_fusion
  1.4 0.1 copy.16
  1.5 0.1 reshape.61
  1.6 0.8 fusion
  2.4 0.1 select_reduce_fusion
  2.6 0.6 pad_add_fusion.table_ref
  3.2 1.4 %copy.17.w_head_ref = bf16[128,64]{1,0:T(8,128)(2,1)} copy(bf16[128,64]{0,1:T(8,128)(2,1)} %param.16) | data formatting | bytes 32768 | tf_op args[7]
  4.6 116.9 %fused.1 = (f32[6,16,512]{2,1,0:T(8,128)}, f32[6,16]{1,0:T(8,128)}, f32[6,1,128]{2,1,0:T(1,128)}) custom-call(s32[105]{0:T(128)} %pad_add_fusion.table_ref, s32[48]{0:T(128)} %lengths_ref.1, bf16[3,128,128,128]{3,2,1,0:T(8,128)(2,1)} %x_ref.1, s32[48,512]{1,0:T(8,128)} %resolved_ref.1, f32[1,128]{1,0:T(1,128)} %bitcast.2, bf16[128,512]{1,0:T(8,128)(2,1)} %w_in_ref.1, ...), custom_call_target="tpu_custom_call" | custom-call | tf_op jit(solution)/shard_map/fused/pallas_call | solution.py:430
  121.5 1.3 %slice_reduce_fusion = f32[6]{0:T(128)} fusion(f32[6,1,128]{2,1,0:T(1,128)} %get-tuple-element.8), kind=kLoop, calls=%fused_computation.4 | loop fusion | bytes 48 | tf_op jit(solution)/shard_map/slice | solution.py:488
  122.8 1.6 %copy.20 = f32[6,16,512]{2,1,0:T(8,128)} copy(f32[6,16,512]{2,1,0:T(8,128)} %get-tuple-element.12) | data formatting | bytes 393216
  124.4 1.3 %copy.21 = f32[6,16]{1,0:T(8,128)} copy(f32[6,16]{1,0:T(8,128)} %get-tuple-element.13) | data formatting | bytes 768
  (1 shorter events, 0.0 us)

commit v3 on v2

v3 whole, which is shorter than its diff:
```python
import functools
import jax
import jax.numpy as jnp
from jax import lax
from jax.experimental import pallas as pl
from jax.experimental.pallas import tpu as pltpu
from jax.sharding import PartitionSpec as P

EPS = 1e-05
LOG2E = 1.4426950408889634
F32 = jnp.float32
BF16 = jnp.bfloat16
MESH = pl.DeviceIdType.MESH
GROUP = 4
LAG = 2
UNROLL = 4


def fused_kernel(
    tmap_ref,
    lengths_ref,
    x_ref,
    vmap_ref,
    resolved_ref,
    gain_ref,
    w_in_ref,
    w_out_ref,
    w_head_ref,
    bias_ref,
    map_ref,
    res_ref,
    best_ref,
    mix_s,
    w1_s,
    w2_s,
    bias_s,
    cen_s,
    tmw_s,
    weight_s,
    x_s,
    xc_s,
    h_s,
    hd_s,
    rs_s,
    hdc_s,
    rsc_s,
    err_s,
    tm_s,
    tab_v,
    tab_s,
    den_s,
    acc_s,
    sum_s,
    send_s,
    sendt_s,
    recv_s,
    recvt_s,
    yrecv_s,
    yrecvt_s,
    top_s,
    topz_s,
    x_sem,
    tab_sem,
    send_sem,
    sendt_sem,
    recv_sem,
    recvt_sem,
    ysend_sem,
    ysendt_sem,
    yrecv_sem,
    yrecvt_sem,
    topsend_sem,
    topz_sem,
    *,
    blocks,
    parts,
    n_cplx,
):
    slots, side, _, chan = x_ref.shape
    bins = bias_ref.shape[1]
    lanes = 128
    rows = side // parts
    cpx_dev = map_ref.shape[0]
    cells = cpx_dev * blocks
    tile = lax.axis_index("tile")
    mine = lax.axis_index("cplx")
    by = tile // parts
    bz = lax.rem(tile, parts)
    device = tile * n_cplx + mine
    last = parts - 1

    def whole_div(n, d):
        return ((n * (65536 // d + 1)) >> 16) if d > 1 else n

    def x_copy(s, j):
        p = lax.rem(bz + last - s, parts)
        return pltpu.make_async_copy(
            x_ref.at[j, pl.ds(p * rows, rows)],
            x_s.at[pl.ds((s * slots + j) * rows, rows)],
            x_sem.at[s, j],
        )

    def x_start(s, carry):
        for j in range(slots):
            x_copy(s, j).start()
        return carry

    lax.fori_loop(0, parts, x_start, 0)

    barrier = pltpu.get_barrier_semaphore()
    plane = parts * n_cplx

    def greet(d, carry):
        other = lax.rem(bz * n_cplx + mine + d, plane)
        pl.semaphore_signal(
            barrier,
            inc=1,
            device_id=(by * parts + other // n_cplx, lax.rem(other, n_cplx)),
            device_id_type=MESH,
        )
        return carry

    lax.fori_loop(1, plane, greet, 0)
    for d in range(1, blocks):
        pl.semaphore_signal(
            barrier,
            inc=1,
            device_id=(lax.rem(by + d, blocks) * parts + bz, mine),
            device_id_type=MESH,
        )

    r = lax.broadcasted_iota(jnp.int32, (chan, chan), 0)
    c = lax.broadcasted_iota(jnp.int32, (chan, chan), 1)
    mix_s[0:chan, :] = (jnp.where(r == c, 1.0, 0.0) - 1.0 / chan).astype(BF16)
    mix_s[chan : chan + bins, :] = w_head_ref[...]
    w1_s[...] = (w_in_ref[...].astype(F32).T * gain_ref[...]).astype(BF16)
    w2_s[...] = lax.dot_general(
        w_head_ref[...], w_out_ref[...], (((1,), (1,)), ((), ())), preferred_element_type=F32
    ).astype(BF16)
    bias_s[...] = jnp.broadcast_to(bias_ref[...] * LOG2E, (lanes, bins)).T
    b = lax.broadcasted_iota(jnp.int32, (bins, lanes), 0).astype(F32)
    cen_s[...] = (b + 0.5) * (31.0 / (bins - 2))
    pos = lax.broadcasted_iota(jnp.int32, (1, side), 1)

    def stage_a(group, par):
        row = pl.multiple_of(group * GROUP, GROUP)
        x = x_s[pl.ds(row, GROUP), :, :].reshape(GROUP * side, chan)
        first = lax.dot_general(
            mix_s[...], x, (((1,), (1,)), ((), ())), preferred_element_type=F32
        )
        xc = first[:chan]
        var = jnp.mean(xc * xc, axis=0, keepdims=True)
        xc_s[par] = xc.astype(BF16)
        rs_s[par] = lax.rsqrt(var + EPS) * LOG2E
        bias = jnp.concatenate([bias_s[...]] * GROUP, axis=1)
        hd_s[par] = first[chan:] * LOG2E + bias

    def stage_b(par):
        z = jnp.dot(w1_s[...], xc_s[par], preferred_element_type=F32)
        h_s[par] = jnp.maximum(z, 0.0).astype(BF16)
        hdc_s[par] = hd_s[par]
        rsc_s[par] = rs_s[par]

    def stage_c(row, slot, par):
        cen = jnp.concatenate([cen_s[...]] * GROUP, axis=1)
        tmw = jnp.concatenate([tmw_s[slot]] * GROUP, axis=1)
        y = jnp.dot(w2_s[...], h_s[par], preferred_element_type=F32)
        logits = hdc_s[par] + rsc_s[par] * y
        top = jnp.max(logits, axis=0, keepdims=True)
        e = jnp.exp2(logits - top)
        s0 = jnp.sum(e, axis=0, keepdims=True)
        s1 = jnp.sum(e * cen, axis=0, keepdims=True)
        s2 = jnp.sum(e * tmw, axis=0, keepdims=True)
        inv = 1.0 / s0
        expected = s1 * inv
        term = s2 * inv
        for i in range(GROUP):
            err_s[pl.ds(row + i, 1), :] = expected[:, i * side : (i + 1) * side]
            tm_s[pl.ds(row + i, 1), :] = term[:, i * side : (i + 1) * side]

    n = lax.broadcasted_iota(jnp.int32, (1, vmap_ref.shape[1]), 1)
    unit = whole_div(n, slots)
    slot_of = n - unit * slots
    tile_of = whole_div(unit, n_cplx)
    cplx_of = unit - tile_of * n_cplx
    k_all = vmap_ref[0:1, :]
    member = k_all - mine * cpx_dev
    here = (k_all >= 0) & (member >= 0) & (member < cpx_dev)
    key = jnp.where(here, (vmap_ref[1:2, :] * cpx_dev + member) * blocks + vmap_ref[2:3, :], -1)
    near = tile_of - by * parts
    key2 = jnp.where(here & (near >= 0) & (near < parts), near * slots + slot_of, -1)
    want = lax.broadcasted_iota(jnp.int32, (128, n.shape[1]), 0)
    spot = jnp.where(want == key, tile_of * slots + slot_of + 1, 0)
    spot2 = jnp.where(want == key2, cplx_of, 0)
    tab_v[...] = jnp.zeros_like(tab_v)
    for i, wide in enumerate((spot, spot2)):
        folded = jnp.zeros((128, 128), jnp.int32)
        width = wide.shape[1]
        for at in range(0, width, 128):
            piece = wide[:, at : min(at + 128, width)]
            if piece.shape[1] < 128:
                fill = jnp.zeros((128, 128 - piece.shape[1]), jnp.int32)
                piece = jnp.concatenate([piece, fill], axis=1)
            folded = folded + piece
        folded = folded.T
        while folded.shape[0] > 1:
            half = folded.shape[0] // 2
            folded = folded[:half] + folded[half:]
        tab_v[i : i + 1, :] = folded
    tab_copy = pltpu.make_async_copy(tab_v, tab_s, tab_sem.at[0])
    tab_copy.start()

    for j in range(slots):
        x_copy(0, j).wait()
    stage_a(0, 0)
    stage_a(1, 1)
    stage_b(0)
    stage_a(2, 0)

    def valid(k, length, block):
        line = resolved_ref[pl.ds(k, 1), :]
        part = jnp.zeros((1, side), jnp.int32)
        for q in range(blocks):
            part = jnp.where(block == q, line[:, q * side : (q + 1) * side], part)
        return jnp.where((pos + block * side < length) & (part > 0), 1.0, 0.0)

    owners = []
    for j in range(slots):
        at = device * slots + j
        found = tmap_ref[0, at]
        k = jnp.maximum(found, 0)
        length = lengths_ref[k]
        size = jnp.full((bins, lanes), jnp.maximum(length, 19).astype(F32) - 15.0, F32)
        d0 = 1.24 * jnp.exp(jnp.log(size) * (1.0 / 3.0)) - 1.8
        ratio = cen_s[...] / d0
        tmw_s[j] = 1.0 / (1.0 + ratio * ratio)
        row_valid = valid(k, length, jnp.maximum(tmap_ref[1, at], 0))
        col_valid = valid(k, length, jnp.maximum(tmap_ref[2, at], 0))
        col_valid = jnp.where(found >= 0, col_valid, 0.0)
        weight_s[j] = jnp.broadcast_to(row_valid, (side, side)).T * col_valid
        owners.append(jnp.where(found >= 0, whole_div(k, cpx_dev), -1))

    acc_s[...] = jnp.zeros_like(acc_s)
    den_s[...] = jnp.ones_like(den_s)
    for m in range(cpx_dev):
        k = mine * cpx_dev + m
        length = lengths_ref[k]
        line = resolved_ref[pl.ds(k, 1), :]
        where = lax.broadcasted_iota(jnp.int32, line.shape, 1)
        valid_line = jnp.where((where < length) & (line > 0), 1.0, 0.0)
        total = jnp.sum(valid_line, axis=1, keepdims=True)
        for q in range(blocks):
            part = valid_line[:, q * side : (q + 1) * side]
            own = pltpu.roll(part, lax.rem(side - bz * rows, side), 1)
            den_s[q, m : m + 1, :] = jnp.maximum(own * total, 1.0)

    per_stage = slots * rows // GROUP
    per_slot = rows // GROUP
    tm_s[...] = jnp.zeros_like(tm_s)

    def err_copy(s, d):
        p = lax.rem(bz + last - s, parts)
        o = lax.rem(mine + d, n_cplx)
        return pltpu.make_async_remote_copy(
            src_ref=send_s.at[s, o],
            dst_ref=recv_s.at[bz * n_cplx + mine],
            send_sem=send_sem.at[s],
            recv_sem=recv_sem.at[bz],
            device_id=(by * parts + p, o),
            device_id_type=MESH,
        )

    def tm_copy(s, d):
        p = lax.rem(bz + last - s, parts)
        o = lax.rem(mine + d, n_cplx)
        return pltpu.make_async_remote_copy(
            src_ref=sendt_s.at[s],
            dst_ref=recvt_s.at[bz * n_cplx + mine],
            send_sem=sendt_sem.at[s],
            recv_sem=recvt_sem.at[bz],
            device_id=(by * parts + p, o),
            device_id_type=MESH,
        )

    def await_part(zs, count):
        at = recvt_s.at[pl.ds(zs * n_cplx, count)]
        pltpu.make_async_copy(at, at, recvt_sem.at[zs]).wait()
        at = recv_s.at[pl.ds(zs * n_cplx, count)]
        pltpu.make_async_copy(at, at, recv_sem.at[zs]).wait()

    def y_copy(zs, d, small):
        to = lax.rem(by + d, blocks)
        ref, sent, sem = (
            (yrecvt_s, ysendt_sem, yrecvt_sem) if small else (yrecv_s, ysend_sem, yrecv_sem)
        )
        at = pl.ds((by * parts + zs) * slots, slots)
        return pltpu.make_async_remote_copy(
            src_ref=ref.at[at],
            dst_ref=ref.at[at],
            send_sem=sent.at[zs],
            recv_sem=sem.at[by],
            device_id=(to * parts + bz, mine),
            device_id_type=MESH,
        )

    order = sorted(range(1, blocks), key=lambda d: -min(d, blocks - d))

    def forward(s, count):
        zs = lax.rem(bz + s + 1, parts)
        await_part(zs, count)
        from_o = [tab_s[1, zs * slots + j] for j in range(slots)]
        pieces = [jnp.zeros((rows, side), F32)] * slots
        lines = [jnp.zeros((1, rows), F32)] * slots
        for o in range(n_cplx):
            piece = recv_s[zs * n_cplx + o]
            line = recvt_s[zs * n_cplx + o]
            for j in range(slots):
                pieces[j] = jnp.where(from_o[j] == o, piece, pieces[j])
                short = line[:, j * rows : (j + 1) * rows]
                lines[j] = jnp.where(from_o[j] == o, short, lines[j])
        for j in range(slots):
            to = (by * parts + zs) * slots + j
            yrecvt_s[to, :, 0:rows] = lines[j]
            yrecv_s[to] = pieces[j]
        for d in order:
            y_copy(zs, d, True).start()
        for d in order:
            y_copy(zs, d, False).start()

    tab_copy.wait()

    def stage(s, carry):
        @pl.when(s < last)
        def _():
            for j in range(slots):
                x_copy(s + 1, j).wait()

        def body(i, inner):
            g = UNROLL * i
            stop = parts * per_stage - 1
            row = pl.multiple_of(g * GROUP, UNROLL * GROUP)
            for u in range(UNROLL):
                stage_b((u + 1) % 2)
                stage_c(row + u * GROUP, (g + u) // per_slot, u % 2)
                stage_a(jnp.minimum(s * per_stage + g + u + 3, stop), (u + 1) % 2)
            return inner

        lax.fori_loop(0, per_stage // UNROLL, body, 0)

        p = lax.rem(bz + last - s, parts)
        start = pl.multiple_of(p * rows, rows)
        errs = []
        for j in range(slots):
            weight = weight_s[j, pl.ds(start, rows), :]
            errs.append(err_s[j * rows : (j + 1) * rows, :] * weight)
            tm_s[j * rows : (j + 1) * rows, :] = tm_s[j * rows : (j + 1) * rows, :] * weight
        sendt_s[s] = jnp.sum(tm_s[...].T, axis=0, keepdims=True)
        for o in range(n_cplx):
            piece = jnp.zeros_like(errs[0])
            for j in range(slots):
                piece = jnp.where(owners[j] == o, errs[j], piece)
            send_s[s, o] = piece

        @pl.when(s == 0)
        def _():
            pl.semaphore_wait(barrier, plane - 1 + blocks - 1)

        for d in range(1, n_cplx):
            tm_copy(s, d).start()
        for d in range(1, n_cplx):
            err_copy(s, d).start()

        @pl.when(s < last)
        def _():
            tm_copy(s, 0).start()
            err_copy(s, 0).start()

        @pl.when(s == last)
        def _():
            recv_s[bz * n_cplx + mine] = send_s[s, mine]
            recvt_s[bz * n_cplx + mine] = sendt_s[s]

        @pl.when(s >= LAG)
        def _():
            forward(s - LAG, n_cplx)

        return carry

    lax.fori_loop(0, parts, stage, 0)
    for s in range(max(parts - LAG, 0), parts):
        forward(s, n_cplx if s < last else n_cplx - 1)

    def y_wait(ref, sem, ys):
        at = ref.at[pl.ds(ys * parts * slots, parts * slots)]
        pltpu.make_async_copy(at, at, sem.at[ys]).wait()

    for d in range(1, blocks):
        y_wait(yrecvt_s, yrecvt_sem, lax.rem(by + d, blocks))

    for q in range(blocks):
        for m in range(cpx_dev):
            acc = jnp.zeros((1, rows), F32)
            for e in range(blocks):
                found = tab_s[0, (q * cpx_dev + m) * blocks + e]
                line = yrecvt_s[jnp.clip(found - 1, 0, blocks * parts * slots - 1)][:, 0:rows]
                acc = acc + jnp.where(found > 0, line, 0.0)
            acc_s[q, m : m + 1, 0:rows] = acc
    top_s[...] = jnp.max(acc_s[...] / den_s[...], axis=0)

    def top_copy(d):
        return pltpu.make_async_remote_copy(
            src_ref=top_s,
            dst_ref=topz_s.at[bz],
            send_sem=topsend_sem.at[d],
            recv_sem=topz_sem.at[bz],
            device_id=(by * parts + lax.rem(bz + d, parts), mine),
            device_id_type=MESH,
        )

    for d in sorted(range(1, parts), key=lambda d: -min(d, parts - d)):
        top_copy(d).start()

    for d in range(1, blocks):
        y_wait(yrecv_s, yrecv_sem, lax.rem(by + d, blocks))
    for m in range(cpx_dev):
        total = jnp.zeros((rows, side), F32)
        for q in range(blocks):
            found = tab_s[0, (by * cpx_dev + m) * blocks + q]
            piece = jnp.where(found > 0, yrecv_s[jnp.clip(found - 1, 0, blocks * parts * slots - 1)], 0.0)
            map_ref[m, :, q * side : (q + 1) * side] = piece
            total = total + piece
        sum_s[m * rows : (m + 1) * rows, :] = total
    totals = jnp.sum(sum_s[...].T, axis=0, keepdims=True)
    for m in range(cpx_dev):
        denom = den_s[by, m : m + 1, 0:rows]
        res_ref[m : m + 1, :] = totals[:, m * rows : (m + 1) * rows] / denom

    best = top_s[...]
    for d in range(1, parts):
        zs = lax.rem(bz + d, parts)
        pltpu.make_async_copy(topz_s.at[zs], topz_s.at[zs], topz_sem.at[zs]).wait()
        best = jnp.maximum(best, topz_s[zs])
    best = jnp.max(best, axis=1, keepdims=True)
    best_ref[...] = jnp.broadcast_to(best, best_ref.shape)

    def drain(s, count):
        at = send_s.at[s, pl.ds(0, count)]
        pltpu.make_async_copy(at, at, send_sem.at[s]).wait()
        at = recvt_s.at[pl.ds(0, count)]
        pltpu.make_async_copy(at, at, sendt_sem.at[s]).wait()

    def drain_all(s, carry):
        drain(s, n_cplx)
        return carry

    lax.fori_loop(0, last, drain_all, 0)
    drain(last, n_cplx - 1)

    def drain_y(zs, carry):
        at = pl.ds(0, (blocks - 1) * slots)
        pltpu.make_async_copy(yrecvt_s.at[at], yrecvt_s.at[at], ysendt_sem.at[zs]).wait()
        pltpu.make_async_copy(yrecv_s.at[at], yrecv_s.at[at], ysend_sem.at[zs]).wait()
        return carry

    lax.fori_loop(0, parts, drain_y, 0)
    for d in range(1, parts):
        top_copy(d).wait_send()


def shards(pair_tiles, tile_map, lengths, resolved, ln_gain, w_in, w_out, w_head, head_bias):
    n_tile = lax.axis_size("tile")
    n_cplx = lax.axis_size("cplx")
    slots, side, _, chan = pair_tiles.shape
    hid = w_in.shape[1]
    bins = w_head.shape[1]
    complexes, maxres = resolved.shape
    blocks = maxres // side
    cpx_dev = complexes // n_cplx
    rows = maxres // n_tile
    parts = side // rows
    cells = cpx_dev * blocks
    vmem = pl.BlockSpec(memory_space=pltpu.VMEM)
    smem = pl.BlockSpec(memory_space=pltpu.SMEM)
    dma = pltpu.SemaphoreType.DMA
    groups = GROUP * side
    error_map, residue, best = pl.pallas_call(
        functools.partial(fused_kernel, blocks=blocks, parts=parts, n_cplx=n_cplx),
        in_specs=[smem, smem, pl.BlockSpec(memory_space=pl.ANY)] + [vmem] * 7,
        out_specs=[vmem] * 3,
        out_shape=[
            jax.ShapeDtypeStruct((cpx_dev, rows, maxres), F32),
            jax.ShapeDtypeStruct((cpx_dev, rows), F32),
            jax.ShapeDtypeStruct((8, 128), F32),
        ],
        scratch_shapes=[
            pltpu.VMEM((chan + bins, chan), BF16),
            pltpu.VMEM((hid, chan), BF16),
            pltpu.VMEM((bins, hid), BF16),
            pltpu.VMEM((bins, 128), F32),
            pltpu.VMEM((bins, 128), F32),
            pltpu.VMEM((slots, bins, 128), F32),
            pltpu.VMEM((slots, side, side), F32),
            pltpu.VMEM((parts * slots * rows, side, chan), BF16),
            pltpu.VMEM((2, chan, groups), BF16),
            pltpu.VMEM((2, hid, groups), BF16),
            pltpu.VMEM((2, bins, groups), F32),
            pltpu.VMEM((2, 1, groups), F32),
            pltpu.VMEM((2, bins, groups), F32),
            pltpu.VMEM((2, 1, groups), F32),
            pltpu.VMEM((slots * rows, side), F32),
            pltpu.VMEM((128, side), F32),
            pltpu.VMEM((8, 128), jnp.int32),
            pltpu.SMEM((8, 128), jnp.int32),
            pltpu.VMEM((blocks, 8, 128), F32),
            pltpu.VMEM((blocks, 8, 128), F32),
            pltpu.VMEM((128, side), F32),
            pltpu.VMEM((parts, n_cplx, rows, side), F32),
            pltpu.VMEM((parts, 1, 128), F32),
            pltpu.VMEM((parts * n_cplx, rows, side), F32),
            pltpu.VMEM((parts * n_cplx, 1, 128), F32),
            pltpu.VMEM((blocks * parts * slots, rows, side), F32),
            pltpu.VMEM((blocks * parts * slots, 1, 128), F32),
            pltpu.VMEM((8, 128), F32),
            pltpu.VMEM((parts, 8, 128), F32),
            dma((parts, slots)),
            dma((1,)),
            dma((parts,)),
            dma((parts,)),
            dma((parts,)),
            dma((parts,)),
            dma((parts,)),
            dma((parts,)),
            dma((blocks,)),
            dma((blocks,)),
            dma((parts,)),
            dma((parts,)),
        ],
        compiler_params=pltpu.CompilerParams(
            collective_id=0, has_side_effects=True, vmem_limit_bytes=60 * 1024 * 1024
        ),
        name="fused",
    )(
        tile_map.T,
        lengths,
        pair_tiles,
        tile_map.T,
        resolved,
        ln_gain.reshape(1, chan),
        w_in,
        w_out,
        w_head.T,
        head_bias.reshape(1, bins),
    )
    return error_map, residue, best[:cpx_dev, 0]


def solution(mesh):
    placed = (P(("tile", "cplx"), None, None, None), P(), P(), P(), P(), P(), P(), P(), P())
    return jax.shard_map(
        shards,
        mesh=mesh,
        in_specs=placed,
        out_specs=(P("cplx", "tile", None), P("cplx", "tile"), P("cplx")),
        check_vma=False,
    )
```

time: 126 us -> 63.6 us (0.50)
  Pallas kernels: 117 us -> 58.3 us
  local copies, waits for them, and re-layouts: 6.57 us -> 4.18 us
  other arithmetic: 1.56 us -> 0 us
    pallas_call x1, Pallas kernels: 117 us -> 58.3 us  [shards(): pl.pallas_call(functools.partial(fused_kernel, blocks=blocks, parts=parts...]
    unnamed x3 -> x2, local copies, waits for them, and re-layouts: 4.31 us -> 2.88 us
where the time goes in v3:
time: 63.6 us; the launch traced here: 63.1 us
  Pallas kernels  58.3 us (92%)
  local copies, waits for them, and re-layouts  4.18 us (7%)
  between operations  0.64 us (1%)
    pallas_call x1, Pallas kernels, shards(): pl.pallas_call(functools.partial(fused_kernel, blocks=blocks, parts=parts...  58.3 us
    unnamed x2, local copies, waits for them, and re-layouts  2.88 us
    slice x1, local copies, waits for them, and re-layouts, shards(): return (error_map, residue, best[:cpx_dev, 0])  1.3 us

profile of v3, /device:TPU:32, one launch (start us, length us, event | category | flops | bytes accessed | tf_op | source)
XLA Modules:
  0.0 63.1 jit_solution(4586033301899419561)
XLA Ops:
  0.6 58.3 %fused.1 = (f32[6,16,512]{2,1,0:T(8,128)}, f32[6,16]{1,0:T(8,128)}, f32[8,128]{1,0:T(8,128)}) custom-call(s32[3,768]{1,0:T(4,128)} %bitcast.4, s32[48]{0:T(128)} %lengths_ref.1, bf16[3,128,128,128]{3,2,1,0:T(8,128)(2,1)} %x_ref.1, s32[3,768]{1,0:T(4,128)} %bitcast.5, s32[48,512]{1,0:T(8,128)} %resolved_ref.1, f32[1,128]{1,0:T(1,128)} %bitcast.7, ...), custom_call_target="tpu_custom_call" | custom-call | tf_op jit(solution)/shard_map/fused/pallas_call | solution.py:486
  58.9 1.3 %slice_reduce_fusion = f32[6]{0:T(128)} fusion(f32[8,128]{1,0:T(8,128)} %get-tuple-element.8), kind=kLoop, calls=%fused_computation | loop fusion | bytes 48 | tf_op jit(solution)/shard_map/slice | solution.py:554
  60.2 1.6 %copy.14 = f32[6,16,512]{2,1,0:T(8,128)} copy(f32[6,16,512]{2,1,0:T(8,128)} %get-tuple-element.12) | data formatting | bytes 393216
  61.8 1.3 %copy.15 = f32[6,16]{1,0:T(8,128)} copy(f32[6,16]{1,0:T(8,128)} %get-tuple-element.13) | data formatting | bytes 768

commit v4 on v3

--- a/solution.py
+++ b/solution.py
@@ -11,9 +11,9 @@
 F32 = jnp.float32
 BF16 = jnp.bfloat16
 MESH = pl.DeviceIdType.MESH
-GROUP = 4
-LAG = 2
-UNROLL = 4
+GROUP = 8
+LAG = 3
+UNROLL = 6
 
 
 def fused_kernel(
@@ -92,8 +92,11 @@
     def whole_div(n, d):
         return ((n * (65536 // d + 1)) >> 16) if d > 1 else n
 
+    def offset(s):
+        return parts // 2 + (1 - 2 * (s & 1)) * ((s + 1) >> 1)
+
     def x_copy(s, j):
-        p = lax.rem(bz + last - s, parts)
+        p = lax.rem(bz + offset(s), parts)
         return pltpu.make_async_copy(
             x_ref.at[j, pl.ds(p * rows, rows)],
             x_s.at[pl.ds((s * slots + j) * rows, rows)],
@@ -110,17 +113,15 @@
     barrier = pltpu.get_barrier_semaphore()
     plane = parts * n_cplx
 
-    def greet(d, carry):
-        other = lax.rem(bz * n_cplx + mine + d, plane)
-        pl.semaphore_signal(
-            barrier,
-            inc=1,
-            device_id=(by * parts + other // n_cplx, lax.rem(other, n_cplx)),
-            device_id_type=MESH,
-        )
-        return carry
-
-    lax.fori_loop(1, plane, greet, 0)
+    for dz in range(parts):
+        to = by * parts + lax.rem(bz + dz, parts)
+        for d in range(1 if dz == 0 else 0, n_cplx):
+            pl.semaphore_signal(
+                barrier,
+                inc=1,
+                device_id=(to, lax.rem(mine + d, n_cplx)),
+                device_id_type=MESH,
+            )
     for d in range(1, blocks):
         pl.semaphore_signal(
             barrier,
@@ -259,7 +260,7 @@
     tm_s[...] = jnp.zeros_like(tm_s)
 
     def err_copy(s, d):
-        p = lax.rem(bz + last - s, parts)
+        p = lax.rem(bz + offset(s), parts)
         o = lax.rem(mine + d, n_cplx)
         return pltpu.make_async_remote_copy(
             src_ref=send_s.at[s, o],
@@ -271,7 +272,7 @@
         )
 
     def tm_copy(s, d):
-        p = lax.rem(bz + last - s, parts)
+        p = lax.rem(bz + offset(s), parts)
         o = lax.rem(mine + d, n_cplx)
         return pltpu.make_async_remote_copy(
             src_ref=sendt_s.at[s],
@@ -306,7 +307,7 @@
     order = sorted(range(1, blocks), key=lambda d: -min(d, blocks - d))
 
     def forward(s, count):
-        zs = lax.rem(bz + s + 1, parts)
+        zs = lax.rem(bz + parts - offset(s), parts)
         await_part(zs, count)
         from_o = [tab_s[1, zs * slots + j] for j in range(slots)]
         pieces = [jnp.zeros((rows, side), F32)] * slots
@@ -347,7 +348,7 @@
 
         lax.fori_loop(0, per_stage // UNROLL, body, 0)
 
-        p = lax.rem(bz + last - s, parts)
+        p = lax.rem(bz + offset(s), parts)
         start = pl.multiple_of(p * rows, rows)
         errs = []
         for j in range(slots):
@@ -440,8 +441,10 @@
         zs = lax.rem(bz + d, parts)
         pltpu.make_async_copy(topz_s.at[zs], topz_s.at[zs], topz_sem.at[zs]).wait()
         best = jnp.maximum(best, topz_s[zs])
-    best = jnp.max(best, axis=1, keepdims=True)
-    best_ref[...] = jnp.broadcast_to(best, best_ref.shape)
+    best = jnp.broadcast_to(jnp.max(best, axis=1, keepdims=True), (8, lanes))
+    down = lax.broadcasted_iota(jnp.int32, (8, lanes), 0)
+    across = lax.broadcasted_iota(jnp.int32, (8, lanes), 1)
+    best_ref[...] = jnp.sum(jnp.where(down == across, best, 0.0), axis=0, keepdims=True)
 
     def drain(s, count):
         at = send_s.at[s, pl.ds(0, count)]
@@ -465,6 +468,12 @@
     lax.fori_loop(0, parts, drain_y, 0)
     for d in range(1, parts):
         top_copy(d).wait_send()
+
+
+def hand_out(map_in, res_in, best_in, map_ref, res_ref, best_ref):
+    map_ref[...] = map_in[...]
+    res_ref[...] = res_in[...]
+    best_ref[...] = best_in[:, 0 : best_ref.shape[1]]
 
 
 def shards(pair_tiles, tile_map, lengths, resolved, ln_gain, w_in, w_out, w_head, head_bias):
@@ -490,7 +499,7 @@
         out_shape=[
             jax.ShapeDtypeStruct((cpx_dev, rows, maxres), F32),
             jax.ShapeDtypeStruct((cpx_dev, rows), F32),
-            jax.ShapeDtypeStruct((8, 128), F32),
+            jax.ShapeDtypeStruct((1, 128), F32),
         ],
         scratch_shapes=[
             pltpu.VMEM((chan + bins, chan), BF16),
@@ -551,7 +560,18 @@
         w_head.T,
         head_bias.reshape(1, bins),
     )
-    return error_map, residue, best[:cpx_dev, 0]
+    error_map, residue, best = pl.pallas_call(
+        hand_out,
+        in_specs=[vmem] * 3,
+        out_specs=[vmem] * 3,
+        out_shape=[
+            jax.ShapeDtypeStruct(error_map.shape, F32),
+            jax.ShapeDtypeStruct(residue.shape, F32),
+            jax.ShapeDtypeStruct((1, cpx_dev), F32),
+        ],
+        name="hand_out",
+    )(error_map, residue, best)
+    return error_map, residue, best.reshape(cpx_dev)
 
 
 def solution(mesh):

time: 63.6 us -> 56.7 us (0.89)
  local copies, waits for them, and re-layouts: 4.18 us -> 0 us
  Pallas kernels: 58.3 us -> 55.6 us
    pallas_call x1, Pallas kernels: 58.3 us -> 54 us  [shards(): pl.pallas_call(functools.partial(fused_kernel, blocks=blocks, parts=parts...]
    unnamed x2 -> x0, local copies, waits for them, and re-layouts: 2.88 us -> none
    pallas_call x0 -> x1, Pallas kernels: none -> 1.63 us  [shards(): pl.pallas_call(hand_out, in_specs=[vmem] * 3, out_specs=[vmem] * 3, out_s...]
    slice x1 -> x0, local copies, waits for them, and re-layouts: 1.3 us -> none  [shards(): return (error_map, residue, best[:cpx_dev, 0])]
where the time goes in v4:
time: 56.7 us; the launch traced here: 56.2 us
  Pallas kernels  55.6 us (98%)
  between operations  0.64 us (1%)
    pallas_call x1, Pallas kernels, shards(): pl.pallas_call(functools.partial(fused_kernel, blocks=blocks, parts=parts...  54 us
    pallas_call x1, Pallas kernels, shards(): pl.pallas_call(hand_out, in_specs=[vmem] * 3, out_specs=[vmem] * 3, out_s...  1.63 us

profile of v4, /device:TPU:32, one launch (start us, length us, event | category | flops | bytes accessed | tf_op | source)
XLA Modules:
  0.0 56.2 jit_solution(1771652374556717318)
XLA Ops:
  0.6 54.0 %fused.1 = (f32[6,16,512]{2,1,0:T(8,128)}, f32[6,16]{1,0:T(8,128)}, f32[1,128]{1,0:T(1,128)}) custom-call(s32[3,768]{1,0:T(4,128)} %bitcast.5, s32[48]{0:T(128)} %lengths_ref.1, bf16[3,128,128,128]{3,2,1,0:T(8,128)(2,1)} %x_ref.1, s32[3,768]{1,0:T(4,128)} %bitcast.6, s32[48,512]{1,0:T(8,128)} %resolved_ref.1, f32[1,128]{1,0:T(1,128)} %bitcast.8, ...), custom_call_target="tpu_custom_call" | custom-call | tf_op jit(solution)/shard_map/fused/pallas_call | solution.py:495
  54.6 1.6 %hand_out.1 = (f32[6,16,512]{2,1,0:T(8,128)}, f32[6,16]{1,0:T(8,128)}, f32[1,6]{1,0:T(1,128)}) custom-call(f32[6,16,512]{2,1,0:T(8,128)} %get-tuple-element.9.map_in, f32[6,16]{1,0:T(8,128)} %get-tuple-element.10.res_in, f32[1,128]{1,0:T(1,128)} %get-tuple-element.11.best_in), custom_call_target="tpu_custom_call" | custom-call | tf_op jit(solution)/shard_map/hand_out/pallas_call | solution.py:563

commit v5 on v4

--- a/solution.py
+++ b/solution.py
@@ -17,9 +17,20 @@
 
 
 def fused_kernel(
+    tmap_h,
+    lengths_h,
+    x_ref,
+    resolved_h,
+    gain_h,
+    w_in_h,
+    w_out_h,
+    w_head_h,
+    bias_h,
+    map_ref,
+    res_ref,
+    best_ref,
     tmap_ref,
     lengths_ref,
-    x_ref,
     vmap_ref,
     resolved_ref,
     gain_ref,
@@ -27,9 +38,7 @@
     w_out_ref,
     w_head_ref,
     bias_ref,
-    map_ref,
-    res_ref,
-    best_ref,
+    in_sem,
     mix_s,
     w1_s,
     w2_s,
@@ -42,8 +51,6 @@
     h_s,
     hd_s,
     rs_s,
-    hdc_s,
-    rsc_s,
     err_s,
     tm_s,
     tab_v,
@@ -77,7 +84,7 @@
     n_cplx,
 ):
     slots, side, _, chan = x_ref.shape
-    bins = bias_ref.shape[1]
+    bins = bias_h.shape[1]
     lanes = 128
     rows = side // parts
     cpx_dev = map_ref.shape[0]
@@ -108,7 +115,26 @@
             x_copy(s, j).start()
         return carry
 
-    lax.fori_loop(0, parts, x_start, 0)
+    def bring(i):
+        pairs = (
+            (w_head_h, w_head_ref),
+            (bias_h, bias_ref),
+            (w_in_h, w_in_ref),
+            (gain_h, gain_ref),
+            (w_out_h, w_out_ref),
+            (tmap_h, vmap_ref),
+            (tmap_h, tmap_ref),
+            (lengths_h, lengths_ref),
+            (resolved_h, resolved_ref),
+        )
+        return pltpu.make_async_copy(*pairs[i], in_sem.at[i])
+
+    bring(0).start()
+    for j in range(slots):
+        x_copy(0, j).start()
+    for i in range(1, 9):
+        bring(i).start()
+    lax.fori_loop(1, parts, x_start, 0)
 
     barrier = pltpu.get_barrier_semaphore()
     plane = parts * n_cplx
@@ -130,6 +156,8 @@
             device_id_type=MESH,
         )
 
+    for i in range(9):
+        bring(i).wait()
     r = lax.broadcasted_iota(jnp.int32, (chan, chan), 0)
     c = lax.broadcasted_iota(jnp.int32, (chan, chan), 1)
     mix_s[0:chan, :] = (jnp.where(r == c, 1.0, 0.0) - 1.0 / chan).astype(BF16)
@@ -143,7 +171,7 @@
     cen_s[...] = (b + 0.5) * (31.0 / (bins - 2))
     pos = lax.broadcasted_iota(jnp.int32, (1, side), 1)
 
-    def stage_a(group, par):
+    def stage_a(group, par, keep):
         row = pl.multiple_of(group * GROUP, GROUP)
         x = x_s[pl.ds(row, GROUP), :, :].reshape(GROUP * side, chan)
         first = lax.dot_general(
@@ -152,21 +180,19 @@
         xc = first[:chan]
         var = jnp.mean(xc * xc, axis=0, keepdims=True)
         xc_s[par] = xc.astype(BF16)
-        rs_s[par] = lax.rsqrt(var + EPS) * LOG2E
+        rs_s[keep] = lax.rsqrt(var + EPS) * LOG2E
         bias = jnp.concatenate([bias_s[...]] * GROUP, axis=1)
-        hd_s[par] = first[chan:] * LOG2E + bias
+        hd_s[keep] = first[chan:] * LOG2E + bias
 
     def stage_b(par):
         z = jnp.dot(w1_s[...], xc_s[par], preferred_element_type=F32)
         h_s[par] = jnp.maximum(z, 0.0).astype(BF16)
-        hdc_s[par] = hd_s[par]
-        rsc_s[par] = rs_s[par]
-
-    def stage_c(row, slot, par):
+
+    def stage_c(row, slot, par, keep):
         cen = jnp.concatenate([cen_s[...]] * GROUP, axis=1)
         tmw = jnp.concatenate([tmw_s[slot]] * GROUP, axis=1)
         y = jnp.dot(w2_s[...], h_s[par], preferred_element_type=F32)
-        logits = hdc_s[par] + rsc_s[par] * y
+        logits = hd_s[keep] + rs_s[keep] * y
         top = jnp.max(logits, axis=0, keepdims=True)
         e = jnp.exp2(logits - top)
         s0 = jnp.sum(e, axis=0, keepdims=True)
@@ -211,12 +237,13 @@
     tab_copy = pltpu.make_async_copy(tab_v, tab_s, tab_sem.at[0])
     tab_copy.start()
 
-    for j in range(slots):
+    x_copy(0, 0).wait()
+    stage_a(0, 0, 0)
+    stage_a(1, 1, 1)
+    for j in range(1, slots):
         x_copy(0, j).wait()
-    stage_a(0, 0)
-    stage_a(1, 1)
     stage_b(0)
-    stage_a(2, 0)
+    stage_a(2, 0, 2)
 
     def valid(k, length, block):
         line = resolved_ref[pl.ds(k, 1), :]
@@ -342,8 +369,8 @@
             row = pl.multiple_of(g * GROUP, UNROLL * GROUP)
             for u in range(UNROLL):
                 stage_b((u + 1) % 2)
-                stage_c(row + u * GROUP, (g + u) // per_slot, u % 2)
-                stage_a(jnp.minimum(s * per_stage + g + u + 3, stop), (u + 1) % 2)
+                stage_c(row + u * GROUP, (g + u) // per_slot, u % 2, u % 3)
+                stage_a(jnp.minimum(s * per_stage + g + u + 3, stop), (u + 1) % 2, u % 3)
             return inner
 
         lax.fori_loop(0, per_stage // UNROLL, body, 0)
@@ -489,12 +516,11 @@
     parts = side // rows
     cells = cpx_dev * blocks
     vmem = pl.BlockSpec(memory_space=pltpu.VMEM)
-    smem = pl.BlockSpec(memory_space=pltpu.SMEM)
     dma = pltpu.SemaphoreType.DMA
     groups = GROUP * side
     error_map, residue, best = pl.pallas_call(
         functools.partial(fused_kernel, blocks=blocks, parts=parts, n_cplx=n_cplx),
-        in_specs=[smem, smem, pl.BlockSpec(memory_space=pl.ANY)] + [vmem] * 7,
+        in_specs=[pl.BlockSpec(memory_space=pl.ANY)] * 9,
         out_specs=[vmem] * 3,
         out_shape=[
             jax.ShapeDtypeStruct((cpx_dev, rows, maxres), F32),
@@ -502,6 +528,16 @@
             jax.ShapeDtypeStruct((1, 128), F32),
         ],
         scratch_shapes=[
+            pltpu.SMEM((3, tile_map.shape[0]), jnp.int32),
+            pltpu.SMEM((complexes,), jnp.int32),
+            pltpu.VMEM((3, tile_map.shape[0]), jnp.int32),
+            pltpu.VMEM((complexes, maxres), jnp.int32),
+            pltpu.VMEM((1, chan), F32),
+            pltpu.VMEM((chan, hid), BF16),
+            pltpu.VMEM((hid, chan), BF16),
+            pltpu.VMEM((bins, chan), BF16),
+            pltpu.VMEM((1, bins), F32),
+            dma((9,)),
             pltpu.VMEM((chan + bins, chan), BF16),
             pltpu.VMEM((hid, chan), BF16),
             pltpu.VMEM((bins, hid), BF16),
@@ -512,10 +548,8 @@
             pltpu.VMEM((parts * slots * rows, side, chan), BF16),
             pltpu.VMEM((2, chan, groups), BF16),
             pltpu.VMEM((2, hid, groups), BF16),
-            pltpu.VMEM((2, bins, groups), F32),
-            pltpu.VMEM((2, 1, groups), F32),
-            pltpu.VMEM((2, bins, groups), F32),
-            pltpu.VMEM((2, 1, groups), F32),
+            pltpu.VMEM((3, bins, groups), F32),
+            pltpu.VMEM((3, 1, groups), F32),
             pltpu.VMEM((slots * rows, side), F32),
             pltpu.VMEM((128, side), F32),
             pltpu.VMEM((8, 128), jnp.int32),
@@ -545,14 +579,13 @@
             dma((parts,)),
         ],
         compiler_params=pltpu.CompilerParams(
-            collective_id=0, has_side_effects=True, vmem_limit_bytes=60 * 1024 * 1024
+            collective_id=0, has_side_effects=True, vmem_limit_bytes=67043328
         ),
         name="fused",
     )(
         tile_map.T,
         lengths,
         pair_tiles,
-        tile_map.T,
         resolved,
         ln_gain.reshape(1, chan),
         w_in,

time: 56.7 us -> 55.8 us (0.984)
  Pallas kernels: 55.6 us -> 54.5 us
    pallas_call x1, Pallas kernels: 54 us -> 52.9 us  [shards(): pl.pallas_call(functools.partial(fused_kernel, blocks=blocks, parts=parts...]
where the time goes in v5:
time: 55.8 us; the launch traced here: 55.2 us
  Pallas kernels  54.5 us (98%)
  between operations  0.64 us (1%)
    pallas_call x1, Pallas kernels, shards(): pl.pallas_call(functools.partial(fused_kernel, blocks=blocks, parts=parts...  52.9 us
    pallas_call x1, Pallas kernels, shards(): pl.pallas_call(hand_out, in_specs=[vmem] * 3, out_specs=[vmem] * 3, out_s...  1.63 us

profile of v5, /device:TPU:32, one launch (start us, length us, event | category | flops | bytes accessed | tf_op | source)
XLA Modules:
  0.0 55.2 jit_solution(306932271147619610)
XLA Ops:
  0.6 52.9 %fused.1 = (f32[6,16,512]{2,1,0:T(8,128)}, f32[6,16]{1,0:T(8,128)}, f32[1,128]{1,0:T(1,128)}) custom-call(s32[3,768]{1,0:T(4,128)} %bitcast.6, s32[48]{0:T(128)} %lengths_h.1, bf16[3,128,128,128]{3,2,1,0:T(8,128)(2,1)} %x_ref.1, s32[48,512]{1,0:T(8,128)} %resolved_h.1, f32[1,128]{1,0:T(1,128)} %bitcast.7, bf16[128,512]{1,0:T(8,128)(2,1)} %w_in_h.1, ...), custom_call_target="tpu_custom_call" | custom-call | tf_op jit(solution)/shard_map/fused/pallas_call | solution.py:521
  53.5 1.6 %hand_out.1 = (f32[6,16,512]{2,1,0:T(8,128)}, f32[6,16]{1,0:T(8,128)}, f32[1,6]{1,0:T(1,128)}) custom-call(f32[6,16,512]{2,1,0:T(8,128)} %get-tuple-element.9.map_in, f32[6,16]{1,0:T(8,128)} %get-tuple-element.10.res_in, f32[1,128]{1,0:T(1,128)} %get-tuple-element.11.best_in), custom_call_target="tpu_custom_call" | custom-call | tf_op jit(solution)/shard_map/hand_out/pallas_call | solution.py:596

commit v6 on v5

--- a/solution.py
+++ b/solution.py
@@ -310,12 +310,6 @@
             device_id_type=MESH,
         )
 
-    def await_part(zs, count):
-        at = recvt_s.at[pl.ds(zs * n_cplx, count)]
-        pltpu.make_async_copy(at, at, recvt_sem.at[zs]).wait()
-        at = recv_s.at[pl.ds(zs * n_cplx, count)]
-        pltpu.make_async_copy(at, at, recv_sem.at[zs]).wait()
-
     def y_copy(zs, d, small):
         to = lax.rem(by + d, blocks)
         ref, sent, sem = (
@@ -333,27 +327,38 @@
 
     order = sorted(range(1, blocks), key=lambda d: -min(d, blocks - d))
 
-    def forward(s, count):
+    def forward_tm(s, count):
         zs = lax.rem(bz + parts - offset(s), parts)
-        await_part(zs, count)
-        from_o = [tab_s[1, zs * slots + j] for j in range(slots)]
-        pieces = [jnp.zeros((rows, side), F32)] * slots
+        at = recvt_s.at[pl.ds(zs * n_cplx, count)]
+        pltpu.make_async_copy(at, at, recvt_sem.at[zs]).wait()
         lines = [jnp.zeros((1, rows), F32)] * slots
         for o in range(n_cplx):
-            piece = recv_s[zs * n_cplx + o]
             line = recvt_s[zs * n_cplx + o]
             for j in range(slots):
-                pieces[j] = jnp.where(from_o[j] == o, piece, pieces[j])
                 short = line[:, j * rows : (j + 1) * rows]
-                lines[j] = jnp.where(from_o[j] == o, short, lines[j])
+                lines[j] = jnp.where(tab_s[1, zs * slots + j] == o, short, lines[j])
         for j in range(slots):
-            to = (by * parts + zs) * slots + j
-            yrecvt_s[to, :, 0:rows] = lines[j]
-            yrecv_s[to] = pieces[j]
+            yrecvt_s[(by * parts + zs) * slots + j, :, 0:rows] = lines[j]
         for d in order:
             y_copy(zs, d, True).start()
+
+    def forward_err(s, count):
+        zs = lax.rem(bz + parts - offset(s), parts)
+        at = recv_s.at[pl.ds(zs * n_cplx, count)]
+        pltpu.make_async_copy(at, at, recv_sem.at[zs]).wait()
+        pieces = [jnp.zeros((rows, side), F32)] * slots
+        for o in range(n_cplx):
+            piece = recv_s[zs * n_cplx + o]
+            for j in range(slots):
+                pieces[j] = jnp.where(tab_s[1, zs * slots + j] == o, piece, pieces[j])
+        for j in range(slots):
+            yrecv_s[(by * parts + zs) * slots + j] = pieces[j]
         for d in order:
             y_copy(zs, d, False).start()
+
+    def forward(s, count):
+        forward_tm(s, count)
+        forward_err(s, count)
 
     tab_copy.wait()
 

time: 55.8 us -> 55.3 us (level)
  no operation moved by 1% of the time
where the time goes in v6:
time: 55.3 us; the launch traced here: 55 us
  Pallas kernels  54.4 us (98%)
  between operations  0.64 us (1%)
    pallas_call x1, Pallas kernels, shards(): pl.pallas_call(functools.partial(fused_kernel, blocks=blocks, parts=parts...  52.8 us
    pallas_call x1, Pallas kernels, shards(): pl.pallas_call(hand_out, in_specs=[vmem] * 3, out_specs=[vmem] * 3, out_s...  1.63 us

profile of v6, /device:TPU:32, one launch (start us, length us, event | category | flops | bytes accessed | tf_op | source)
XLA Modules:
  0.0 55.0 jit_solution(9608505485355568931)
XLA Ops:
  0.6 52.8 %fused.1 = (f32[6,16,512]{2,1,0:T(8,128)}, f32[6,16]{1,0:T(8,128)}, f32[1,128]{1,0:T(1,128)}) custom-call(s32[3,768]{1,0:T(4,128)} %bitcast.6, s32[48]{0:T(128)} %lengths_h.1, bf16[3,128,128,128]{3,2,1,0:T(8,128)(2,1)} %x_ref.1, s32[48,512]{1,0:T(8,128)} %resolved_h.1, f32[1,128]{1,0:T(1,128)} %bitcast.7, bf16[128,512]{1,0:T(8,128)(2,1)} %w_in_h.1, ...), custom_call_target="tpu_custom_call" | custom-call | tf_op jit(solution)/shard_map/fused/pallas_call | solution.py:526
  53.4 1.6 %hand_out.1 = (f32[6,16,512]{2,1,0:T(8,128)}, f32[6,16]{1,0:T(8,128)}, f32[1,6]{1,0:T(1,128)}) custom-call(f32[6,16,512]{2,1,0:T(8,128)} %get-tuple-element.9.map_in, f32[6,16]{1,0:T(8,128)} %get-tuple-element.10.res_in, f32[1,128]{1,0:T(1,128)} %get-tuple-element.11.best_in), custom_call_target="tpu_custom_call" | custom-call | tf_op jit(solution)/shard_map/hand_out/pallas_call | solution.py:601
